TPU v7x, 32 devices: a whole 2x2x4 slice. The times are simulated.
32 devices in a mesh: gx: 4 (over z), gy: 2 (over y), gz: 4 (over x, core).
Axes of the slice: x: 2, y: 2, z: 4, core: 2. Of those that a mesh axis runs over, the one named last changes fastest.
Arguments:
- state: float32 [9, 64, 32, 512], P(None, 'gx', 'gy', 'gz'), may hold values from 0 to 1
- mobility: float32 [8], replicated, may hold values from 0.5 to 2
- seeds: int32 [2, 2, 64, 32], replicated, may hold values from 0 to 8
- frame_shifts: int32 [2], replicated, may hold values from 0 to 2, as said below
Outputs:
- state_out: float32 [9, 64, 32, 512], P(None, 'gx', 'gy', 'gz')
Inputs may be any that keep to these rules, and one draw needn't show every extreme that they name: A value of 8 seeds no grain in that cell. `frame_shifts`: the frame advances 2 planes in at least one step and stays in place in at least one other.
All inputs are finite; a program needn't handle non-finite values.
Results may differ from a plain program's by a relative error of at most 0.0001.
Values sent between devices are 32-bit elements; how exact they have to be, the bound alone decides.
No kernel may reach another device: no remote copies, remote signals or barrier semaphores. Data moves between devices by JAX's collectives and lax.ppermute only.
A program may use at most 64 MiB of HBM per device.

v0:
```python
import functools

import jax
import jax.numpy as jnp
from jax import lax
from jax.experimental import pallas as pl
from jax.experimental.pallas import tpu as pltpu
from jax.sharding import PartitionSpec as P

step_rate = 0.1
stiffness = 0.7
coupling = 0.5
diffusion = 0.14
rejection = 0.5
nucleus = 0.3
melt_solute = 1.0

TILE = 8
LANES = 128
REACH = 2
GROUP = 6
SHARE = 4

VMEM = pl.BlockSpec(memory_space=pltpu.VMEM)
SMEM = pl.BlockSpec(memory_space=pltpu.SMEM)


def iota(shape, axis):
    return lax.broadcasted_iota(jnp.int32, shape, axis)


def is_even():
    return lax.rem(lax.axis_index("gx"), 2) == 0


def group_and_slot():
    lane = iota((1, LANES), 1)
    slot = lax.shift_right_logical(lane * 43, 8)
    return slot, lane - slot * GROUP


def edge_tile(ref, g, x):
    rows = ref.shape[2]
    low = ref[g, x, 0:TILE]
    high = ref[g, x, rows - TILE : rows]
    return jnp.where(iota((TILE, LANES), 0) < TILE // 2, low, high)


def corner_rows(k):
    row = iota((TILE, LANES), 0)
    return (row == 2 * k) | (row == (2 * k + TILE - 1) % TILE)


def faces_kernel(state, face_a, face_b, sems):
    width = state.shape[1]
    even = is_even()
    last = width - REACH
    copies = [
        pltpu.make_async_copy(
            state.at[:, pl.ds(jnp.where(pick, last, 0), REACH)], face, sems.at[n]
        )
        for n, (pick, face) in enumerate(((jnp.logical_not(even), face_b), (even, face_a)))
    ]
    for copy in copies:
        copy.start()
    for copy in copies:
        copy.wait()


def rims_kernel(state, rows, corner_a, corner_b):
    fields, width = state.shape[:2]
    even = is_even()
    row = iota((TILE, LANES), 0)
    outer = (row < REACH) | (row >= TILE - REACH)
    for g in range(fields):
        for pair in range(width // 2):
            first = edge_tile(state, g, 2 * pair)
            second = edge_tile(state, g, 2 * pair + 1)
            rows[g, pair] = jnp.where(outer, first, pltpu.roll(second, TILE // 2, 0))
    near_a = jnp.where(even, width - 1, 0)
    near_b = jnp.where(even, 0, width - 1)
    for corner, x in ((corner_a, near_a), (corner_b, near_b)):
        for t in range(corner.shape[0]):
            held = None
            for k in range(SHARE):
                g = t * SHARE + k
                if g < fields:
                    tile = edge_tile(state, g, x)
                    if k:
                        tile = jnp.where(corner_rows(k), pltpu.roll(tile, 2 * k, 0), held)
                    held = tile
            corner[t] = held


def bottom_mask(active):
    return jnp.where((iota((1, LANES), 1) == REACH) & active, 0.0, 1.0)


def along(p, mask):
    return pltpu.roll(p, 1, 1) * mask + pltpu.roll(p, LANES - 1, 1)


def early_mask(shifts):
    return bottom_mask((lax.axis_index("gz") == 0) & (shifts[0] > 0))


def slot_shift(slot):
    return (slot * GROUP + REACH) % LANES


def prepare_kernel(state, seeds, shifts, zsum, own, marks):
    fields, width, height, _ = state.shape
    rows = height + TILE
    total_x, total_y = seeds.shape[2:]
    slot, place = group_and_slot()
    mask = early_mask(shifts)
    for g in range(fields):
        held = None
        for x in range(width):
            p = state[g, x]
            zsum[g, x] = along(p, mask)
            moved = pltpu.roll(p, slot_shift(x + REACH), 1)
            held = moved if held is None else jnp.where(slot == x + REACH, moved, held)
        own[g] = held

    step = jnp.where(shifts[0] > 0, 0, 1)
    row_y = iota((rows, total_y), 0)
    y = jnp.where(row_y >= height + TILE // 2, row_y - rows, row_y) + lax.axis_index("gy") * height
    y = jnp.where(y < 0, y + total_y, y)
    y = jnp.where(y >= total_y, y - total_y, y)
    pick_y = jnp.where(iota((rows, total_y), 1) == y, 1.0, 0.0)
    x = slot - REACH + lax.axis_index("gx") * width
    x = jnp.where(x < 0, x + total_x, x)
    x = jnp.where(x >= total_x, x - total_x, x)
    total = jnp.zeros((rows, LANES), jnp.float32)
    for k in range(REACH):
        chosen = seeds[step, k].astype(jnp.float32)
        across = lax.dot_general(
            pick_y, chosen, (((1,), (1,)), ((), ())), preferred_element_type=jnp.float32
        )
        pick_x = jnp.where((iota((total_x, LANES), 0) == x) & (place == REACH + k), 1.0, 0.0)
        total = total + jnp.dot(across, pick_x, preferred_element_type=jnp.float32)
    marks[...] = total


class Halo:
    def __init__(self, merged, face_a, face_b, rest):
        count = 1 if merged else 2
        self.merged = merged
        self.faces = (face_a, face_b)
        self.rows = rest[:count]
        self.corners = (rest[count : 2 * count], rest[2 * count : 3 * count])
        self.even = is_even()

    def both(self, refs, index):
        if self.merged:
            return refs[0][index]
        upper = iota((TILE, LANES), 0) < TILE // 2
        return jnp.where(upper, refs[0][index], refs[1][index])

    def face(self, g, side, n):
        a, b = (ref[g, n] for ref in self.faces)
        return jnp.where(self.even, a, b) if side else jnp.where(self.even, b, a)

    def pair(self, g, n):
        tile = self.both(self.rows, (g, n))
        return tile, pltpu.roll(tile, TILE // 2, 0)

    def corner(self, g, side):
        t, k = g // SHARE, g % SHARE
        a, b = (self.both(refs, (t,)) for refs in self.corners)
        tile = jnp.where(self.even, a, b) if side else jnp.where(self.even, b, a)
        return pltpu.roll(tile, TILE - 2 * k, 0) if k else tile


def slab_kernel(merged, own, face_a, face_b, *rest):
    slab = rest[-1]
    halo = Halo(merged, face_a, face_b, rest[:-1])
    fields, height = own.shape[:2]
    width = 2 * halo.rows[0].shape[1]
    slot, _ = group_and_slot()
    for g in range(fields):
        held = own[g]
        for side in range(2):
            for n in range(REACH):
                where = n + side * (width + REACH)
                moved = pltpu.roll(halo.face(g, side, n), slot_shift(where), 1)
                held = jnp.where(slot == where, moved, held)
        slab[g, 0:height] = held
        tiles = [(REACH - 1, halo.corner(g, 0)), (width + REACH, halo.corner(g, 1))]
        for n in range(width // 2):
            first, second = halo.pair(g, n)
            tiles += [(2 * n + REACH, first), (2 * n + 1 + REACH, second)]
        held = jnp.zeros((TILE, LANES), jnp.float32)
        for where, tile in tiles:
            held = jnp.where(slot == where, pltpu.roll(tile, slot_shift(where), 1), held)
        slab[g, height : height + TILE] = held


def relax(phases, solute, sums, solute_sum, theta, mobility):
    squares = phases[0] * phases[0]
    for phase in phases[1:]:
        squares = squares + phase * phase
    excess = (theta - coupling * solute) - squares
    fresh = []
    fresh_squares = None
    for g, phase in enumerate(phases):
        speed = step_rate * mobility[g]
        rate = speed * excess + (1.0 - 6.0 * stiffness * speed)
        new = phase * rate + (stiffness * speed) * sums[g]()
        fresh.append(new)
        fresh_squares = new * new if fresh_squares is None else fresh_squares + new * new
    kept = (1.0 - 6.0 * diffusion) - rejection * (fresh_squares - squares)
    fresh.append(solute * kept + diffusion * solute_sum())
    return fresh


def bulk_kernel(merged, state, zsum, mobility, shifts, face_a, face_b, *rest):
    done, lower, wide, first, rims, sums, pending = rest[-7:]
    halo = Halo(merged, face_a, face_b, rest[:-7])
    fields, width, height, length = state.shape
    grains = fields - 1
    rows = height + TILE
    top = height + TILE
    span = float(length * lax.axis_size("gz"))
    base = lax.axis_index("gz") * length
    lane = iota((1, LANES), 1)
    slot_of, _ = group_and_slot()
    speeds = [mobility[g] for g in range(grains)]
    own = slice(TILE, TILE + height)

    def theta_of(shift):
        zpos = (base + lane - shift).astype(jnp.float32)
        return 1.0 - 2.0 * (zpos + 0.5) / span

    def put_rim(ref, g, x, tile):
        ref[g, x, 0:TILE] = tile
        ref[g, x, top : top + TILE] = tile

    for g in range(fields):
        for x in range(width):
            wide[g, x + REACH, own] = state[g, x]
        for side in range(2):
            for n in range(REACH):
                wide[g, n + side * (width + REACH), own] = halo.face(g, side, n)
        for n in range(width // 2):
            first_tile, second_tile = halo.pair(g, n)
            put_rim(wide, g, 2 * n + REACH, first_tile)
            put_rim(wide, g, 2 * n + 1 + REACH, second_tile)
        put_rim(wide, g, REACH - 1, halo.corner(g, 0))
        put_rim(wide, g, width + REACH, halo.corner(g, 1))
        for x in (0, width + 2 * REACH - 1):
            put_rim(wide, g, x, jnp.zeros((TILE, LANES), jnp.float32))

    mask_first = early_mask(shifts)
    theta_first = theta_of(shifts[0])

    def lateral(ref, g, x, with_rim):
        total = ref[g, x - 1, own] + ref[g, x + 1, own]
        total = total + ref[g, x, TILE - 1 : top - 1] + ref[g, x, TILE + 1 : top + 1]
        if not with_rim:
            return total
        rim = ref[g, x - 1, 0:TILE] + ref[g, x + 1, 0:TILE]
        rim = rim + ref[g, x, top - 1 : top - 1 + TILE] + ref[g, x, 1 : TILE + 1]
        return jnp.concatenate([total, rim], axis=0)

    def plane_first(x, zsum_own, zsum_rim):
        full = [wide[g, x, TILE : top + TILE] for g in range(fields)]
        parts = [
            lambda g=g: lateral(wide, g, x, True)
            + jnp.concatenate([zsum_own(g), zsum_rim(g)], axis=0)
            for g in range(fields)
        ]
        fresh = relax(full[:grains], full[grains], parts[:grains], parts[grains], theta_first, speeds)
        for g in range(fields):
            first[g, x - 1, own] = fresh[g][0:height]
            put_rim(first, g, x - 1, fresh[g][height:rows])

    def put_lower(slot, source):
        for g in range(fields):
            moved = pltpu.roll(source(g), slot, 1)
            lower[g] = jnp.where(slot_of * GROUP + REACH + 1 == slot, moved, lower[g])

    lower[...] = jnp.zeros_like(lower)
    for x in (1, width + REACH):
        plane_first(
            x,
            lambda g, x=x: along(wide[g, x, own], mask_first),
            lambda g, x=x: along(wide[g, x, 0:TILE], mask_first),
        )
    for g in range(fields):
        rims[0, g] = along(wide[g, REACH, 0:TILE], mask_first)
        sums[0, g] = jnp.zeros((height, LANES), jnp.float32)

    def plane_of(x):
        return lambda g: jnp.concatenate([first[g, x, own], first[g, x, 0:TILE]], axis=0)

    @pl.loop(0, width)
    def _(x):
        now = lax.rem(x, 2)
        put_lower((x + 1) * GROUP + REACH + 1, plane_of(x))
        plane_first(x + REACH, lambda g: zsum[g, x], lambda g: rims[now, g])
        for g in range(fields):
            rims[1 - now, g] = along(wide[g, x + REACH + 1, 0:TILE], mask_first)

    for x in (width, width + 1):
        put_lower((x + 1) * GROUP + REACH + 1, plane_of(x))

    theta_second = theta_of(REACH)
    mask_second = bottom_mask(lax.axis_index("gz") == 0)

    for g in range(fields):
        sums[0, g] = along(first[g, 1, own], mask_second)
        pending[0, g] = jnp.zeros((height, LANES), jnp.float32)

    def flush(now, x):
        for g in range(fields):
            done[g, x] = pltpu.roll(pending[now, g], LANES - REACH, 1)

    @pl.loop(0, width)
    def _(x):
        now = lax.rem(x, 2)
        flush(now, jnp.maximum(x - 1, 0))
        full = [first[g, x + 1, own] for g in range(fields)]
        parts = [
            lambda g=g: lateral(first, g, x + 1, False) + sums[now, g] for g in range(fields)
        ]
        fresh = relax(full[:grains], full[grains], parts[:grains], parts[grains], theta_second, speeds)
        for g in range(fields):
            pending[1 - now, g] = fresh[g]
            sums[1 - now, g] = along(first[g, x + 2, own], mask_second)

    flush(width % 2, width - 1)


def crown_kernel(done, slab, above, lower, marks, mobility, shifts, out, whole, sems):
    fields, rows = slab.shape[:2]
    grains = fields - 1
    width, height, length = done.shape[1:]
    span = float(length * lax.axis_size("gz"))
    base = lax.axis_index("gz") * length
    topmost = lax.axis_index("gz") == lax.axis_size("gz") - 1
    early = shifts[0] > 0
    _, place = group_and_slot()
    speeds = [mobility[g] for g in range(grains)]

    def entering(g):
        if g == grains:
            return jnp.full((rows, LANES), melt_solute, jnp.float32)
        return jnp.where(marks[...] == float(g), nucleus, 0.0)

    planted = (place >= REACH) & (place < 2 * REACH)
    zero = jnp.zeros((rows, LANES), jnp.float32)

    def theta_of(offset):
        zpos = (base + length + place - offset).astype(jnp.float32)
        return 1.0 - 2.0 * (zpos + 0.5) / span

    def around(p):
        total = pltpu.roll(p, GROUP, 1) + pltpu.roll(p, LANES - GROUP, 1)
        total = total + pltpu.roll(p, 1, 0) + pltpu.roll(p, rows - 1, 0)
        return total + pltpu.roll(p, 1, 1) + pltpu.roll(p, LANES - 1, 1)

    def advance(ps, theta):
        sums = [functools.partial(around, p) for p in ps]
        return relax(ps[:grains], ps[grains], sums[:grains], sums[grains], theta, speeds)

    before = []
    for g in range(fields):
        high = jnp.where(topmost, jnp.where(planted & early, entering(g), zero), above[g])
        before.append(jnp.where(place < REACH, slab[g], high))
    middle = advance(before, theta_of(REACH + shifts[0]))
    after = []
    for g in range(fields):
        value = middle[g]
        value = jnp.where(topmost & jnp.logical_not(early) & planted, entering(g), value)
        value = jnp.where(topmost & (place >= 2 * REACH), 0.0, value)
        after.append(jnp.where(place < REACH, lower[g], pltpu.roll(value, 1, 1)))
    final = advance(after, theta_of(REACH + 1 + REACH))

    top = iota((1, LANES), 1) >= LANES - 2 * REACH
    copies = []
    for g in range(fields):
        cut = final[g][0:height]
        for x in range(width):
            shift = (LANES - 2 * REACH - (x + REACH) * GROUP - 1) % LANES
            whole[g, x] = jnp.where(top, pltpu.roll(cut, shift, 1), done[g, x])
        copy = pltpu.make_async_copy(whole.at[g], out.at[g], sems.at[g])
        copy.start()
        copies.append(copy)
    for copy in copies:
        copy.wait()


def shape(*dims):
    return jax.ShapeDtypeStruct(dims, jnp.float32)


def call(kernel, outs, inputs, cost, specs=None, outs_specs=None, scratch=()):
    return pl.pallas_call(
        kernel,
        out_shape=outs,
        in_specs=specs or [VMEM] * len(inputs),
        out_specs=outs_specs or jax.tree.map(lambda _: VMEM, outs),
        scratch_shapes=list(scratch),
        cost_estimate=pl.CostEstimate(flops=cost, bytes_accessed=cost, transcendentals=0),
        compiler_params=pltpu.CompilerParams(vmem_limit_bytes=24 * 1024 * 1024),
    )(*inputs)


def shards(state, mobility, seeds, frame_shifts):
    fields, width, height, length = state.shape
    count_x, count_y, count_z = (lax.axis_size(a) for a in ("gx", "gy", "gz"))
    merged = count_y == 2
    rows = height + TILE
    groups = -(-fields // SHARE)
    block = shape(fields, width, height, length)
    packed = shape(fields, rows, length)

    def partner(i, kind):
        return (i + 1) % count_x if (i % 2 == 0) == (kind == 0) else (i - 1) % count_x

    def swap(value, kind):
        return lax.ppermute(value, "gx", [(i, partner(i, kind)) for i in range(count_x)])

    toward = [-1] if merged else [-1, 1]

    def diagonal(value, kind):
        return [
            lax.ppermute(
                value,
                ("gx", "gy"),
                [
                    (i * count_y + j, partner(i, kind) * count_y + (j + d) % count_y)
                    for i in range(count_x)
                    for j in range(count_y)
                ],
            )
            for d in toward
        ]

    face_a, face_b = call(
        faces_kernel,
        [shape(fields, REACH, height, length)] * 2,
        [state],
        100000,
        specs=[pl.BlockSpec(memory_space=pltpu.HBM)],
        scratch=[pltpu.SemaphoreType.DMA((2,))],
    )
    got_b = swap(face_b, 1)
    edge, corner_a, corner_b = call(
        rims_kernel,
        [
            shape(fields, width // 2, TILE, length),
            shape(groups, TILE, length),
            shape(groups, TILE, length),
        ],
        [state],
        100000,
    )
    near = [
        lax.ppermute(edge, "gy", [(j, (j + d) % count_y) for j in range(count_y)]) for d in toward
    ]
    got_a = swap(face_a, 0)
    far_b = diagonal(corner_b, 1)
    far_a = diagonal(corner_a, 0)
    zsum, own, marks = call(
        prepare_kernel,
        [block, shape(fields, height, length), shape(rows, length)],
        [state, seeds, frame_shifts],
        5000000,
        specs=[VMEM, VMEM, SMEM],
    )
    halo = [got_a, got_b, *near, *far_a, *far_b]
    slab = call(functools.partial(slab_kernel, merged), packed, [own, *halo], 100000)
    above = lax.ppermute(slab, "gz", [(k, k - 1) for k in range(1, count_z)])
    done, lower = call(
        functools.partial(bulk_kernel, merged),
        [block, packed],
        [state, zsum, mobility, frame_shifts, *halo],
        20000000,
        specs=[VMEM, VMEM, SMEM, SMEM] + [VMEM] * len(halo),
        scratch=[
            pltpu.VMEM((fields, width + 2 * REACH, rows + TILE, length), jnp.float32),
            pltpu.VMEM((fields, width + 2, rows + TILE, length), jnp.float32),
            pltpu.VMEM((2, fields, TILE, length), jnp.float32),
            pltpu.VMEM((2, fields, height, length), jnp.float32),
            pltpu.VMEM((2, fields, height, length), jnp.float32),
        ],
    )
    return call(
        crown_kernel,
        block,
        [done, slab, above, lower, marks, mobility, frame_shifts],
        100000,
        specs=[VMEM] * 5 + [SMEM, SMEM],
        outs_specs=pl.BlockSpec(memory_space=pltpu.HBM),
        scratch=[
            pltpu.VMEM((fields, width, height, length), jnp.float32),
            pltpu.SemaphoreType.DMA((fields,)),
        ],
    )


def solution(mesh):
    placed = (P(None, "gx", "gy", "gz"), P(), P(), P())
    return jax.shard_map(
        shards, mesh=mesh, in_specs=placed, out_specs=P(None, "gx", "gy", "gz"), check_vma=False
    )
```

profile of v0, /device:TPU:1, one launch (start us, length us, event | category | flops | bytes accessed | tf_op | source)
XLA Modules:
  0.0 25.5 jit_solution(3856195680323507233)
XLA Ops:
  0.0 0.0 copy-start
  0.0 1.3 %copy-done = f32[9,16,16,128]{3,2,1,0:T(8,128)S(1)} copy-done((f32[9,16,16,128]{3,2,1,0:T(8,128)S(1)}, f32[9,16,16,128]{3,2,1,0:T(8,128)}, u32[]{:S(2)}) %copy-start) | copy-done | bytes 1179672
  1.3 0.0 copy-start.4
  1.3 0.0 copy-start.1
  1.3 0.0 copy-start.2
  1.3 0.1 shard_map.48
  1.3 2.1 %collective-permute-start.2 = (f32[9,8,8,128]{3,2,1,0:T(8,128)S(1)}, f32[9,8,8,128]{3,2,1,0:T(8,128)S(1)}, u32[]{:S(2)}, u32[]{:S(2)}) collective-permute-start(f32[9,8,8,128]{3,2,1,0:T(8,128)S(1)} %get-tuple-element.18), channel_id=1, source_target_pairs={{0,4},{4,0},{1,5},{5,1},{2,6},{6,2},{3,7},{7,3},{8,12},{12,8},{9,1... | collective-permute-start | bytes 884744 | tf_op jit(solution)/shard_map/ppermute | solution.py:462
  3.5 0.1 shard_map.47
  3.5 0.0 copy-start.3
  3.6 1.4 %collective-permute-start = (f32[9,2,16,128]{3,2,1,0:T(8,128)S(1)}, f32[9,2,16,128]{3,2,1,0:T(8,128)S(1)}, u32[]{:S(2)}, u32[]{:S(2)}) collective-permute-start(f32[9,2,16,128]{3,2,1,0:T(8,128)S(1)} %get-tuple-element.16), channel_id=1, source_target_pairs={{0,8},{8,0},{16,24},{24,16},{1,9},{9,1},{17,25},{25,17},{2,10},{10... | collective-permute-start | bytes 442376 | tf_op jit(solution)/shard_map/ppermute | solution.py:424
  4.9 2.2 %collective-permute-start.1 = (f32[9,2,16,128]{3,2,1,0:T(8,128)S(1)}, f32[9,2,16,128]{3,2,1,0:T(8,128)S(1)}, u32[]{:S(2)}, u32[]{:S(2)}) collective-permute-start(f32[9,2,16,128]{3,2,1,0:T(8,128)S(1)} %get-tuple-element.17), channel_id=1, source_target_pairs={{0,24},{8,16},{16,8},{24,0},{1,25},{9,17},{17,9},{25,1},{2,26},{10... | collective-permute-start | bytes 442376 | tf_op jit(solution)/shard_map/ppermute | solution.py:424
  7.1 0.3 %collective-permute-start.3 = (f32[3,8,128]{2,1,0:T(8,128)S(1)}, f32[3,8,128]{2,1,0:T(8,128)S(1)}, u32[]{:S(2)}, u32[]{:S(2)}) collective-permute-start(f32[3,8,128]{2,1,0:T(8,128)S(1)} %get-tuple-element.19), channel_id=1, source_target_pairs={{0,12},{4,8},{8,4},{12,0},{16,28},{20,24},{24,20},{28,16},{1,13},{... | collective-permute-start | bytes 36872 | tf_op jit(solution)/shard_map/ppermute | solution.py:430
  7.5 1.9 %collective-permute-start.4 = (f32[3,8,128]{2,1,0:T(8,128)S(1)}, f32[3,8,128]{2,1,0:T(8,128)S(1)}, u32[]{:S(2)}, u32[]{:S(2)}) collective-permute-start(f32[3,8,128]{2,1,0:T(8,128)S(1)} %get-tuple-element.20), channel_id=1, source_target_pairs={{0,28},{4,24},{8,20},{12,16},{16,12},{20,8},{24,4},{28,0},{1,29},{... | collective-permute-start | bytes 36872 | tf_op jit(solution)/shard_map/ppermute | solution.py:430
  9.3 0.0 copy-done.4
  9.3 0.1 copy.5.seeds
  9.4 0.0 copy-done.1
  9.4 0.0 copy-done.2
  9.4 1.5 %shard_map.46 = (f32[9,16,16,128]{3,2,1,0:T(8,128)S(1)}, f32[9,16,128]{2,1,0:T(8,128)S(1)}, f32[24,128]{1,0:T(8,128)S(1)}) custom-call(f32[9,16,16,128]{3,2,1,0:T(8,128)S(1)} %copy-done.1, s32[2,2,64,32]{3,2,1,0:T(8,128)S(1)} %copy.5.seeds, s32[2]{0:T(128)S(1)} %copy-done.2), custom_call_target="tpu_custom_call" | custom-call | flops 5000000 | bytes 5000000 | tf_op jit(solution)/shard_map/pallas_call | solution.py:400
  11.0 0.1 collective-permute-done.3.rest_1_
  11.1 2.3 %collective-permute-done.4.rest_2_ = f32[3,8,128]{2,1,0:T(8,128)S(1)} collective-permute-done((f32[3,8,128]{2,1,0:T(8,128)S(1)}, f32[3,8,128]{2,1,0:T(8,128)S(1)}, u32[]{:S(2)}, u32[]{:S(2)}) %collective-permute-start.4) | collective-permute-done | bytes 12320 | tf_op jit(solution)/shard_map/ppermute | solution.py:430
  13.4 0.0 collective-permute-done.face_a
  13.4 0.0 collective-permute-done.1.face_b
  13.4 0.0 collective-permute-done.2.rest_0_
  13.4 0.3 %shard_map.50.slab = f32[9,24,128]{2,1,0:T(8,128)S(1)} custom-call(f32[9,16,128]{2,1,0:T(8,128)S(1)} %get-tuple-element.22.own, f32[9,2,16,128]{3,2,1,0:T(8,128)S(1)} %collective-permute-done.face_a, f32[9,2,16,128]{3,2,1,0:T(8,128)S(1)} %collective-permute-done.1.face_b, f32[9,8,8,128]{3,2,1,0:T(8,128)S(1)} %collective-permute-done.2.rest_0_, ...), custom_call_target="tpu_custom_call" | custom-call | flops 100000 | bytes 100000 | tf_op jit(solution)/shard_map/pallas_call | solution.py:400
  13.8 4.1 %collective-permute-start.5 = (f32[9,24,128]{2,1,0:T(8,128)S(1)}, f32[9,24,128]{2,1,0:T(8,128)S(1)}, u32[]{:S(2)}, u32[]{:S(2)}) collective-permute-start(f32[9,24,128]{2,1,0:T(8,128)S(1)} %shard_map.50.slab), channel_id=1, source_target_pairs={{1,0},{2,1},{3,2},{5,4},{6,5},{7,6},{9,8},{10,9},{11,10},{13,12},{... | collective-permute-start | bytes 331784 | tf_op jit(solution)/shard_map/ppermute | solution.py:476
  17.9 0.0 copy-done.3
  17.9 5.6 %shard_map.49 = (f32[9,16,16,128]{3,2,1,0:T(8,128)S(1)}, f32[9,24,128]{2,1,0:T(8,128)S(1)}) custom-call(f32[9,16,16,128]{3,2,1,0:T(8,128)S(1)} %copy-done.1, f32[9,16,16,128]{3,2,1,0:T(8,128)S(1)} %get-tuple-element.15.zsum, f32[8]{0:T(128)S(1)} %copy-done.3, s32[2]{0:T(128)S(1)} %copy-done.2, f32[9,2,16,128]{3,2,1,0:T(8,128)S(1)} %collective-permute-done.face_a, ...), custom_call_target="tpu_custom_call" | custom-call | flops 20000000 | bytes 20000000 | tf_op jit(solution)/shard_map/pallas_call | solution.py:400
  23.5 0.0 collective-permute-done.5.above
  23.5 2.0 %shard_map.51 = f32[9,16,16,128]{3,2,1,0:T(8,128)} custom-call(f32[9,16,16,128]{3,2,1,0:T(8,128)S(1)} %get-tuple-element.21.done, f32[9,24,128]{2,1,0:T(8,128)S(1)} %shard_map.50.slab, f32[9,24,128]{2,1,0:T(8,128)S(1)} %collective-permute-done.5.above, f32[9,24,128]{2,1,0:T(8,128)S(1)} %get-tuple-element.23.lower, f32[24,128]{1,0:T(8,128)S(1)} %get-tuple-element.24.marks, ...), custom_call_target="tpu_custom_call" | custom-call | flops 100000 | bytes 100000 | tf_op jit(solution)/shard_map/pallas_call | solution.py:400
Async XLA Ops:
  0.0 1.3 %copy-start = (f32[9,16,16,128]{3,2,1,0:T(8,128)S(1)}, f32[9,16,16,128]{3,2,1,0:T(8,128)}, u32[]{:S(2)}) copy-start(f32[9,16,16,128]{3,2,1,0:T(8,128)} %state.7) | copy-start | bytes 3538948
  1.3 8.0 %copy-start.4 = (s32[2,2,64,32]{2,3,1,0:T(8,128)S(1)}, s32[2,2,64,32]{2,3,1,0:T(8,128)}, u32[]{:S(2)}) copy-start(s32[2,2,64,32]{2,3,1,0:T(8,128)} %param.6) | copy-start | bytes 98308
  1.3 8.1 %copy-start.1 = (f32[9,16,16,128]{3,2,1,0:T(8,128)S(1)}, f32[9,16,16,128]{3,2,1,0:T(8,128)}, u32[]{:S(2)}) copy-start(f32[9,16,16,128]{3,2,1,0:T(8,128)} %state.7) | copy-start | bytes 3538948
  1.3 8.1 %copy-start.2 = (s32[2]{0:T(128)S(1)}, s32[2]{0:T(128)}, u32[]{:S(2)}) copy-start(s32[2]{0:T(128)} %shifts.5) | copy-start | bytes 28
  1.3 12.1 %collective-permute-start.2 = (f32[9,8,8,128]{3,2,1,0:T(8,128)S(1)}, f32[9,8,8,128]{3,2,1,0:T(8,128)S(1)}, u32[]{:S(2)}, u32[]{:S(2)}) collective-permute-start(f32[9,8,8,128]{3,2,1,0:T(8,128)S(1)} %get-tuple-element.18), channel_id=1, source_target_pairs={{0,4},{4,0},{1,5},{5,1},{2,6},{6,2},{3,7},{7,3},{8,12},{12,8},{9,1... | collective-permute-start | bytes 884744 | tf_op jit(solution)/shard_map/ppermute | solution.py:462
  3.5 14.4 %copy-start.3 = (f32[8]{0:T(128)S(1)}, f32[8]{0:T(128)}, u32[]{:S(2)}) copy-start(f32[8]{0:T(128)} %mobility.3) | copy-start | bytes 100
  3.6 9.9 %collective-permute-start = (f32[9,2,16,128]{3,2,1,0:T(8,128)S(1)}, f32[9,2,16,128]{3,2,1,0:T(8,128)S(1)}, u32[]{:S(2)}, u32[]{:S(2)}) collective-permute-start(f32[9,2,16,128]{3,2,1,0:T(8,128)S(1)} %get-tuple-element.16), channel_id=1, source_target_pairs={{0,8},{8,0},{16,24},{24,16},{1,9},{9,1},{17,25},{25,17},{2,10},{10... | collective-permute-start | bytes 442376 | tf_op jit(solution)/shard_map/ppermute | solution.py:424
  4.9 8.5 %collective-permute-start.1 = (f32[9,2,16,128]{3,2,1,0:T(8,128)S(1)}, f32[9,2,16,128]{3,2,1,0:T(8,128)S(1)}, u32[]{:S(2)}, u32[]{:S(2)}) collective-permute-start(f32[9,2,16,128]{3,2,1,0:T(8,128)S(1)} %get-tuple-element.17), channel_id=1, source_target_pairs={{0,24},{8,16},{16,8},{24,0},{1,25},{9,17},{17,9},{25,1},{2,26},{10... | collective-permute-start | bytes 442376 | tf_op jit(solution)/shard_map/ppermute | solution.py:424
  7.1 4.0 %collective-permute-start.3 = (f32[3,8,128]{2,1,0:T(8,128)S(1)}, f32[3,8,128]{2,1,0:T(8,128)S(1)}, u32[]{:S(2)}, u32[]{:S(2)}) collective-permute-start(f32[3,8,128]{2,1,0:T(8,128)S(1)} %get-tuple-element.19), channel_id=1, source_target_pairs={{0,12},{4,8},{8,4},{12,0},{16,28},{20,24},{24,20},{28,16},{1,13},{... | collective-permute-start | bytes 36872 | tf_op jit(solution)/shard_map/ppermute | solution.py:430
  7.5 6.0 %collective-permute-start.4 = (f32[3,8,128]{2,1,0:T(8,128)S(1)}, f32[3,8,128]{2,1,0:T(8,128)S(1)}, u32[]{:S(2)}, u32[]{:S(2)}) collective-permute-start(f32[3,8,128]{2,1,0:T(8,128)S(1)} %get-tuple-element.20), channel_id=1, source_target_pairs={{0,28},{4,24},{8,20},{12,16},{16,12},{20,8},{24,4},{28,0},{1,29},{... | collective-permute-start | bytes 36872 | tf_op jit(solution)/shard_map/ppermute | solution.py:430
  13.8 9.7 %collective-permute-start.5 = (f32[9,24,128]{2,1,0:T(8,128)S(1)}, f32[9,24,128]{2,1,0:T(8,128)S(1)}, u32[]{:S(2)}, u32[]{:S(2)}) collective-permute-start(f32[9,24,128]{2,1,0:T(8,128)S(1)} %shard_map.50.slab), channel_id=1, source_target_pairs={{1,0},{2,1},{3,2},{5,4},{6,5},{7,6},{9,8},{10,9},{11,10},{13,12},{... | collective-permute-start | bytes 331784 | tf_op jit(solution)/shard_map/ppermute | solution.py:476
where the time goes:
time: 25.6 us; the launch traced here: 25.5 us
  starting transfers between devices  12 us (47%)
  Pallas kernels  9.53 us (37%)
  waiting for transfers between devices  2.49 us (10%)
  local copies, waits for them, and re-layouts  1.38 us (5%)
    pallas_call x6, Pallas kernels, call(): pl.pallas_call(kernel, out_shape=outs, in_specs=specs or [VMEM] * len(inp...  9.53 us
    ppermute x1, starting transfers between devices, shards(): above = lax.ppermute(slab, 'gz', [(k, k - 1) for k in range(1, count_z)])  4.12 us
    ppermute x2, starting transfers between devices, swap(): lax.ppermute(value, 'gx', [(i, partner(i, kind)) for i in range(count_x)])  3.56 us
    ppermute x2, waiting for transfers between devices, diagonal(): lax.ppermute(value, ('gx', 'gy'), [(i * count_y + j, partner(i, kind) * c...  2.48 us
    ppermute x2, starting transfers between devices, diagonal(): lax.ppermute(value, ('gx', 'gy'), [(i * count_y + j, partner(i, kind) * c...  2.2 us
    ppermute x1, starting transfers between devices, shards(): lax.ppermute(edge, 'gy', [(j, (j + d) % count_y) for j in range(count_y)])  2.12 us
    unnamed x11, local copies, waits for them, and re-layouts  1.38 us
  transfers between devices with their start and end apart: 6, of which 2 were waited for; matrix products, arithmetic and copies ran while one was open for 0% of the time, Pallas kernels for 28%

commit v1 on v0

--- a/solution.py
+++ b/solution.py
@@ -6,6 +6,7 @@
 from jax.experimental import pallas as pl
 from jax.experimental.pallas import tpu as pltpu
 from jax.sharding import PartitionSpec as P
+
 
 step_rate = 0.1
 stiffness = 0.7
@@ -20,6 +21,7 @@
 REACH = 2
 GROUP = 6
 SHARE = 4
+UNROLL = 8
 
 VMEM = pl.BlockSpec(memory_space=pltpu.VMEM)
 SMEM = pl.BlockSpec(memory_space=pltpu.SMEM)
@@ -216,8 +218,9 @@
 
 
 def bulk_kernel(merged, state, zsum, mobility, shifts, face_a, face_b, *rest):
-    done, lower, wide, first, rims, sums, pending = rest[-7:]
-    halo = Halo(merged, face_a, face_b, rest[:-7])
+    done, lower, wide, first = rest[-10:-6]
+    rims, sums, pending = rest[-6:-4], rest[-4:-2], rest[-2:]
+    halo = Halo(merged, face_a, face_b, rest[:-10])
     fields, width, height, length = state.shape
     grains = fields - 1
     rows = height + TILE
@@ -289,19 +292,20 @@
             lambda g, x=x: along(wide[g, x, 0:TILE], mask_first),
         )
     for g in range(fields):
-        rims[0, g] = along(wide[g, REACH, 0:TILE], mask_first)
-        sums[0, g] = jnp.zeros((height, LANES), jnp.float32)
+        rims[0][g] = along(wide[g, REACH, 0:TILE], mask_first)
 
     def plane_of(x):
         return lambda g: jnp.concatenate([first[g, x, own], first[g, x, 0:TILE]], axis=0)
 
-    @pl.loop(0, width)
-    def _(x):
-        now = lax.rem(x, 2)
-        put_lower((x + 1) * GROUP + REACH + 1, plane_of(x))
-        plane_first(x + REACH, lambda g: zsum[g, x], lambda g: rims[now, g])
-        for g in range(fields):
-            rims[1 - now, g] = along(wide[g, x + REACH + 1, 0:TILE], mask_first)
+    @pl.loop(0, width // UNROLL)
+    def _(block):
+        for part in range(UNROLL):
+            x = block * UNROLL + part
+            now, after = rims[part % 2], rims[1 - part % 2]
+            put_lower((x + 1) * GROUP + REACH + 1, plane_of(x))
+            plane_first(x + REACH, lambda g: zsum[g, x], lambda g: now[g])
+            for g in range(fields):
+                after[g] = along(wide[g, x + REACH + 1, 0:TILE], mask_first)
 
     for x in (width, width + 1):
         put_lower((x + 1) * GROUP + REACH + 1, plane_of(x))
@@ -310,27 +314,31 @@
     mask_second = bottom_mask(lax.axis_index("gz") == 0)
 
     for g in range(fields):
-        sums[0, g] = along(first[g, 1, own], mask_second)
-        pending[0, g] = jnp.zeros((height, LANES), jnp.float32)
-
-    def flush(now, x):
+        sums[0][g] = along(first[g, 1, own], mask_second)
+        pending[1][g] = jnp.zeros((height, LANES), jnp.float32)
+
+    def flush(held, x):
         for g in range(fields):
-            done[g, x] = pltpu.roll(pending[now, g], LANES - REACH, 1)
-
-    @pl.loop(0, width)
-    def _(x):
-        now = lax.rem(x, 2)
-        flush(now, jnp.maximum(x - 1, 0))
-        full = [first[g, x + 1, own] for g in range(fields)]
-        parts = [
-            lambda g=g: lateral(first, g, x + 1, False) + sums[now, g] for g in range(fields)
-        ]
-        fresh = relax(full[:grains], full[grains], parts[:grains], parts[grains], theta_second, speeds)
-        for g in range(fields):
-            pending[1 - now, g] = fresh[g]
-            sums[1 - now, g] = along(first[g, x + 2, own], mask_second)
-
-    flush(width % 2, width - 1)
+            done[g, x] = pltpu.roll(held[g], LANES - REACH, 1)
+
+    @pl.loop(0, width // UNROLL)
+    def _(block):
+        for part in range(UNROLL):
+            x = block * UNROLL + part
+            now, after = part % 2, 1 - part % 2
+            flush(pending[after], jnp.maximum(x - 1, 0))
+            full = [first[g, x + 1, own] for g in range(fields)]
+            parts = [
+                lambda g=g: lateral(first, g, x + 1, False) + sums[now][g] for g in range(fields)
+            ]
+            fresh = relax(
+                full[:grains], full[grains], parts[:grains], parts[grains], theta_second, speeds
+            )
+            for g in range(fields):
+                pending[now][g] = fresh[g]
+                sums[after][g] = along(first[g, x + 2, own], mask_second)
+
+    flush(pending[1], width - 1)
 
 
 def crown_kernel(done, slab, above, lower, marks, mobility, shifts, out, whole, sems):
@@ -396,7 +404,7 @@
     return jax.ShapeDtypeStruct(dims, jnp.float32)
 
 
-def call(kernel, outs, inputs, cost, specs=None, outs_specs=None, scratch=()):
+def call(kernel, outs, inputs, cost, specs=None, outs_specs=None, scratch=(), grant=24 << 20):
     return pl.pallas_call(
         kernel,
         out_shape=outs,
@@ -404,7 +412,7 @@
         out_specs=outs_specs or jax.tree.map(lambda _: VMEM, outs),
         scratch_shapes=list(scratch),
         cost_estimate=pl.CostEstimate(flops=cost, bytes_accessed=cost, transcendentals=0),
-        compiler_params=pltpu.CompilerParams(vmem_limit_bytes=24 * 1024 * 1024),
+        compiler_params=pltpu.CompilerParams(vmem_limit_bytes=grant),
     )(*inputs)
 
 
@@ -459,7 +467,8 @@
         100000,
     )
     near = [
-        lax.ppermute(edge, "gy", [(j, (j + d) % count_y) for j in range(count_y)]) for d in toward
+        lax.ppermute(edge, "gy", [(j, (j + d) % count_y) for j in range(count_y)])
+        for d in toward
     ]
     got_a = swap(face_a, 0)
     far_b = diagonal(corner_b, 1)
@@ -483,10 +492,9 @@
         scratch=[
             pltpu.VMEM((fields, width + 2 * REACH, rows + TILE, length), jnp.float32),
             pltpu.VMEM((fields, width + 2, rows + TILE, length), jnp.float32),
-            pltpu.VMEM((2, fields, TILE, length), jnp.float32),
-            pltpu.VMEM((2, fields, height, length), jnp.float32),
-            pltpu.VMEM((2, fields, height, length), jnp.float32),
-        ],
+        ]
+        + [pltpu.VMEM((fields, TILE, length), jnp.float32)] * 2
+        + [pltpu.VMEM((fields, height, length), jnp.float32)] * 4,
     )
     return call(
         crown_kernel,

time: 25.6 us -> 23.6 us (0.922)
  Pallas kernels: 9.53 us -> 7.1 us
  waiting for transfers between devices: 2.49 us -> 2.85 us
    pallas_call x6, Pallas kernels: 9.53 us -> 7.1 us  [call(): pl.pallas_call(kernel, out_shape=outs, in_specs=specs or [VMEM] * len(inp...]
    ppermute x1, waiting for transfers between devices: 0.01 us -> 0.36 us  [shards(): above = lax.ppermute(slab, 'gz', [(k, k - 1) for k in range(1, count_z)])]
  transfers between devices with their start and end apart: 6 -> 6, of which waited for: 2 -> 3; matrix products, arithmetic and copies ran while one was open for 0% -> 0% of each run, Pallas kernels for 28% -> 20%
where the time goes in v1:
time: 23.6 us; the launch traced here: 23.4 us
  starting transfers between devices  12 us (51%)
  Pallas kernels  7.1 us (30%)
  waiting for transfers between devices  2.85 us (12%)
  local copies, waits for them, and re-layouts  1.38 us (6%)
    pallas_call x6, Pallas kernels, call(): pl.pallas_call(kernel, out_shape=outs, in_specs=specs or [VMEM] * len(inp...  7.1 us
    ppermute x1, starting transfers between devices, shards(): above = lax.ppermute(slab, 'gz', [(k, k - 1) for k in range(1, count_z)])  4.12 us
    ppermute x2, starting transfers between devices, swap(): lax.ppermute(value, 'gx', [(i, partner(i, kind)) for i in range(count_x)])  3.56 us
    ppermute x2, waiting for transfers between devices, diagonal(): lax.ppermute(value, ('gx', 'gy'), [(i * count_y + j, partner(i, kind) * c...  2.48 us
    ppermute x2, starting transfers between devices, diagonal(): lax.ppermute(value, ('gx', 'gy'), [(i * count_y + j, partner(i, kind) * c...  2.2 us
    ppermute x1, starting transfers between devices, shards(): lax.ppermute(edge, 'gy', [(j, (j + d) % count_y) for j in range(count_y)])  2.12 us
    unnamed x11, local copies, waits for them, and re-layouts  1.38 us
  transfers between devices with their start and end apart: 6, of which 3 were waited for; matrix products, arithmetic and copies ran while one was open for 0% of the time, Pallas kernels for 20%

profile of v1, /device:TPU:1, one launch (start us, length us, event | category | flops | bytes accessed | tf_op | source)
XLA Modules:
  0.0 23.4 jit_solution(887301919537129541)
XLA Ops:
  0.0 0.0 copy-start
  0.0 1.3 %copy-done = f32[9,16,16,128]{3,2,1,0:T(8,128)S(1)} copy-done((f32[9,16,16,128]{3,2,1,0:T(8,128)S(1)}, f32[9,16,16,128]{3,2,1,0:T(8,128)}, u32[]{:S(2)}) %copy-start) | copy-done | bytes 1179672
  1.3 0.0 copy-start.4
  1.3 0.0 copy-start.1
  1.3 0.0 copy-start.2
  1.3 0.1 shard_map.48
  1.3 2.1 %collective-permute-start.2 = (f32[9,8,8,128]{3,2,1,0:T(8,128)S(1)}, f32[9,8,8,128]{3,2,1,0:T(8,128)S(1)}, u32[]{:S(2)}, u32[]{:S(2)}) collective-permute-start(f32[9,8,8,128]{3,2,1,0:T(8,128)S(1)} %get-tuple-element.18), channel_id=1, source_target_pairs={{0,4},{4,0},{1,5},{5,1},{2,6},{6,2},{3,7},{7,3},{8,12},{12,8},{9,1... | collective-permute-start | bytes 884744 | tf_op jit(solution)/shard_map/ppermute | solution.py:470
  3.5 0.1 shard_map.47
  3.5 0.0 copy-start.3
  3.6 1.4 %collective-permute-start = (f32[9,2,16,128]{3,2,1,0:T(8,128)S(1)}, f32[9,2,16,128]{3,2,1,0:T(8,128)S(1)}, u32[]{:S(2)}, u32[]{:S(2)}) collective-permute-start(f32[9,2,16,128]{3,2,1,0:T(8,128)S(1)} %get-tuple-element.16), channel_id=1, source_target_pairs={{0,8},{8,0},{16,24},{24,16},{1,9},{9,1},{17,25},{25,17},{2,10},{10... | collective-permute-start | bytes 442376 | tf_op jit(solution)/shard_map/ppermute | solution.py:432
  4.9 2.2 %collective-permute-start.1 = (f32[9,2,16,128]{3,2,1,0:T(8,128)S(1)}, f32[9,2,16,128]{3,2,1,0:T(8,128)S(1)}, u32[]{:S(2)}, u32[]{:S(2)}) collective-permute-start(f32[9,2,16,128]{3,2,1,0:T(8,128)S(1)} %get-tuple-element.17), channel_id=1, source_target_pairs={{0,24},{8,16},{16,8},{24,0},{1,25},{9,17},{17,9},{25,1},{2,26},{10... | collective-permute-start | bytes 442376 | tf_op jit(solution)/shard_map/ppermute | solution.py:432
  7.1 0.3 %collective-permute-start.3 = (f32[3,8,128]{2,1,0:T(8,128)S(1)}, f32[3,8,128]{2,1,0:T(8,128)S(1)}, u32[]{:S(2)}, u32[]{:S(2)}) collective-permute-start(f32[3,8,128]{2,1,0:T(8,128)S(1)} %get-tuple-element.19), channel_id=1, source_target_pairs={{0,12},{4,8},{8,4},{12,0},{16,28},{20,24},{24,20},{28,16},{1,13},{... | collective-permute-start | bytes 36872 | tf_op jit(solution)/shard_map/ppermute | solution.py:438
  7.5 1.9 %collective-permute-start.4 = (f32[3,8,128]{2,1,0:T(8,128)S(1)}, f32[3,8,128]{2,1,0:T(8,128)S(1)}, u32[]{:S(2)}, u32[]{:S(2)}) collective-permute-start(f32[3,8,128]{2,1,0:T(8,128)S(1)} %get-tuple-element.20), channel_id=1, source_target_pairs={{0,28},{4,24},{8,20},{12,16},{16,12},{20,8},{24,4},{28,0},{1,29},{... | collective-permute-start | bytes 36872 | tf_op jit(solution)/shard_map/ppermute | solution.py:438
  9.3 0.0 copy-done.4
  9.3 0.1 copy.5.seeds
  9.4 0.0 copy-done.1
  9.4 0.0 copy-done.2
  9.4 1.5 %shard_map.46 = (f32[9,16,16,128]{3,2,1,0:T(8,128)S(1)}, f32[9,16,128]{2,1,0:T(8,128)S(1)}, f32[24,128]{1,0:T(8,128)S(1)}) custom-call(f32[9,16,16,128]{3,2,1,0:T(8,128)S(1)} %copy-done.1, s32[2,2,64,32]{3,2,1,0:T(8,128)S(1)} %copy.5.seeds, s32[2]{0:T(128)S(1)} %copy-done.2), custom_call_target="tpu_custom_call" | custom-call | flops 5000000 | bytes 5000000 | tf_op jit(solution)/shard_map/pallas_call | solution.py:408
  11.0 0.1 collective-permute-done.3.rest_1_
  11.1 2.3 %collective-permute-done.4.rest_2_ = f32[3,8,128]{2,1,0:T(8,128)S(1)} collective-permute-done((f32[3,8,128]{2,1,0:T(8,128)S(1)}, f32[3,8,128]{2,1,0:T(8,128)S(1)}, u32[]{:S(2)}, u32[]{:S(2)}) %collective-permute-start.4) | collective-permute-done | bytes 12320 | tf_op jit(solution)/shard_map/ppermute | solution.py:438
  13.4 0.0 collective-permute-done.face_a
  13.4 0.0 collective-permute-done.1.face_b
  13.4 0.0 collective-permute-done.2.rest_0_
  13.4 0.3 %shard_map.50.slab = f32[9,24,128]{2,1,0:T(8,128)S(1)} custom-call(f32[9,16,128]{2,1,0:T(8,128)S(1)} %get-tuple-element.22.own, f32[9,2,16,128]{3,2,1,0:T(8,128)S(1)} %collective-permute-done.face_a, f32[9,2,16,128]{3,2,1,0:T(8,128)S(1)} %collective-permute-done.1.face_b, f32[9,8,8,128]{3,2,1,0:T(8,128)S(1)} %collective-permute-done.2.rest_0_, ...), custom_call_target="tpu_custom_call" | custom-call | flops 100000 | bytes 100000 | tf_op jit(solution)/shard_map/pallas_call | solution.py:408
  13.8 4.1 %collective-permute-start.5 = (f32[9,24,128]{2,1,0:T(8,128)S(1)}, f32[9,24,128]{2,1,0:T(8,128)S(1)}, u32[]{:S(2)}, u32[]{:S(2)}) collective-permute-start(f32[9,24,128]{2,1,0:T(8,128)S(1)} %shard_map.50.slab), channel_id=1, source_target_pairs={{1,0},{2,1},{3,2},{5,4},{6,5},{7,6},{9,8},{10,9},{11,10},{13,12},{... | collective-permute-start | bytes 331784 | tf_op jit(solution)/shard_map/ppermute | solution.py:485
  17.9 0.0 copy-done.3
  17.9 3.1 %shard_map.49 = (f32[9,16,16,128]{3,2,1,0:T(8,128)S(1)}, f32[9,24,128]{2,1,0:T(8,128)S(1)}) custom-call(f32[9,16,16,128]{3,2,1,0:T(8,128)S(1)} %copy-done.1, f32[9,16,16,128]{3,2,1,0:T(8,128)S(1)} %get-tuple-element.15.zsum, f32[8]{0:T(128)S(1)} %copy-done.3, s32[2]{0:T(128)S(1)} %copy-done.2, f32[9,2,16,128]{3,2,1,0:T(8,128)S(1)} %collective-permute-done.face_a, ...), custom_call_target="tpu_custom_call" | custom-call | flops 20000000 | bytes 20000000 | tf_op jit(solution)/shard_map/pallas_call | solution.py:408
  21.0 0.4 %collective-permute-done.5.above = f32[9,24,128]{2,1,0:T(8,128)S(1)} collective-permute-done((f32[9,24,128]{2,1,0:T(8,128)S(1)}, f32[9,24,128]{2,1,0:T(8,128)S(1)}, u32[]{:S(2)}, u32[]{:S(2)}) %collective-permute-start.5) | collective-permute-done | bytes 110624 | tf_op jit(solution)/shard_map/ppermute | solution.py:485
  21.4 2.0 %shard_map.51 = f32[9,16,16,128]{3,2,1,0:T(8,128)} custom-call(f32[9,16,16,128]{3,2,1,0:T(8,128)S(1)} %get-tuple-element.21.done, f32[9,24,128]{2,1,0:T(8,128)S(1)} %shard_map.50.slab, f32[9,24,128]{2,1,0:T(8,128)S(1)} %collective-permute-done.5.above, f32[9,24,128]{2,1,0:T(8,128)S(1)} %get-tuple-element.23.lower, f32[24,128]{1,0:T(8,128)S(1)} %get-tuple-element.24.marks, ...), custom_call_target="tpu_custom_call" | custom-call | flops 100000 | bytes 100000 | tf_op jit(solution)/shard_map/pallas_call | solution.py:408
Async XLA Ops:
  0.0 1.3 %copy-start = (f32[9,16,16,128]{3,2,1,0:T(8,128)S(1)}, f32[9,16,16,128]{3,2,1,0:T(8,128)}, u32[]{:S(2)}) copy-start(f32[9,16,16,128]{3,2,1,0:T(8,128)} %state.7) | copy-start | bytes 3538948
  1.3 8.0 %copy-start.4 = (s32[2,2,64,32]{2,3,1,0:T(8,128)S(1)}, s32[2,2,64,32]{2,3,1,0:T(8,128)}, u32[]{:S(2)}) copy-start(s32[2,2,64,32]{2,3,1,0:T(8,128)} %param.6) | copy-start | bytes 98308
  1.3 8.1 %copy-start.1 = (f32[9,16,16,128]{3,2,1,0:T(8,128)S(1)}, f32[9,16,16,128]{3,2,1,0:T(8,128)}, u32[]{:S(2)}) copy-start(f32[9,16,16,128]{3,2,1,0:T(8,128)} %state.7) | copy-start | bytes 3538948
  1.3 8.1 %copy-start.2 = (s32[2]{0:T(128)S(1)}, s32[2]{0:T(128)}, u32[]{:S(2)}) copy-start(s32[2]{0:T(128)} %shifts.5) | copy-start | bytes 28
  1.3 12.1 %collective-permute-start.2 = (f32[9,8,8,128]{3,2,1,0:T(8,128)S(1)}, f32[9,8,8,128]{3,2,1,0:T(8,128)S(1)}, u32[]{:S(2)}, u32[]{:S(2)}) collective-permute-start(f32[9,8,8,128]{3,2,1,0:T(8,128)S(1)} %get-tuple-element.18), channel_id=1, source_target_pairs={{0,4},{4,0},{1,5},{5,1},{2,6},{6,2},{3,7},{7,3},{8,12},{12,8},{9,1... | collective-permute-start | bytes 884744 | tf_op jit(solution)/shard_map/ppermute | solution.py:470
  3.5 14.4 %copy-start.3 = (f32[8]{0:T(128)S(1)}, f32[8]{0:T(128)}, u32[]{:S(2)}) copy-start(f32[8]{0:T(128)} %mobility.3) | copy-start | bytes 100
  3.6 9.9 %collective-permute-start = (f32[9,2,16,128]{3,2,1,0:T(8,128)S(1)}, f32[9,2,16,128]{3,2,1,0:T(8,128)S(1)}, u32[]{:S(2)}, u32[]{:S(2)}) collective-permute-start(f32[9,2,16,128]{3,2,1,0:T(8,128)S(1)} %get-tuple-element.16), channel_id=1, source_target_pairs={{0,8},{8,0},{16,24},{24,16},{1,9},{9,1},{17,25},{25,17},{2,10},{10... | collective-permute-start | bytes 442376 | tf_op jit(solution)/shard_map/ppermute | solution.py:432
  4.9 8.5 %collective-permute-start.1 = (f32[9,2,16,128]{3,2,1,0:T(8,128)S(1)}, f32[9,2,16,128]{3,2,1,0:T(8,128)S(1)}, u32[]{:S(2)}, u32[]{:S(2)}) collective-permute-start(f32[9,2,16,128]{3,2,1,0:T(8,128)S(1)} %get-tuple-element.17), channel_id=1, source_target_pairs={{0,24},{8,16},{16,8},{24,0},{1,25},{9,17},{17,9},{25,1},{2,26},{10... | collective-permute-start | bytes 442376 | tf_op jit(solution)/shard_map/ppermute | solution.py:432
  7.1 4.0 %collective-permute-start.3 = (f32[3,8,128]{2,1,0:T(8,128)S(1)}, f32[3,8,128]{2,1,0:T(8,128)S(1)}, u32[]{:S(2)}, u32[]{:S(2)}) collective-permute-start(f32[3,8,128]{2,1,0:T(8,128)S(1)} %get-tuple-element.19), channel_id=1, source_target_pairs={{0,12},{4,8},{8,4},{12,0},{16,28},{20,24},{24,20},{28,16},{1,13},{... | collective-permute-start | bytes 36872 | tf_op jit(solution)/shard_map/ppermute | solution.py:438
  7.5 6.0 %collective-permute-start.4 = (f32[3,8,128]{2,1,0:T(8,128)S(1)}, f32[3,8,128]{2,1,0:T(8,128)S(1)}, u32[]{:S(2)}, u32[]{:S(2)}) collective-permute-start(f32[3,8,128]{2,1,0:T(8,128)S(1)} %get-tuple-element.20), channel_id=1, source_target_pairs={{0,28},{4,24},{8,20},{12,16},{16,12},{20,8},{24,4},{28,0},{1,29},{... | collective-permute-start | bytes 36872 | tf_op jit(solution)/shard_map/ppermute | solution.py:438
  13.8 7.6 %collective-permute-start.5 = (f32[9,24,128]{2,1,0:T(8,128)S(1)}, f32[9,24,128]{2,1,0:T(8,128)S(1)}, u32[]{:S(2)}, u32[]{:S(2)}) collective-permute-start(f32[9,24,128]{2,1,0:T(8,128)S(1)} %shard_map.50.slab), channel_id=1, source_target_pairs={{1,0},{2,1},{3,2},{5,4},{6,5},{7,6},{9,8},{10,9},{11,10},{13,12},{... | collective-permute-start | bytes 331784 | tf_op jit(solution)/shard_map/ppermute | solution.py:485

commit v2 on v1

--- a/solution.py
+++ b/solution.py
@@ -53,45 +53,36 @@
     return (row == 2 * k) | (row == (2 * k + TILE - 1) % TILE)
 
 
-def faces_kernel(state, face_a, face_b, sems):
-    width = state.shape[1]
+def load_kernel(state, block, face_a, face_b, rows, corner_a, corner_b, sems):
+    fields, width = state.shape[:2]
     even = is_even()
     last = width - REACH
     copies = [
-        pltpu.make_async_copy(
-            state.at[:, pl.ds(jnp.where(pick, last, 0), REACH)], face, sems.at[n]
-        )
-        for n, (pick, face) in enumerate(((jnp.logical_not(even), face_b), (even, face_a)))
+        pltpu.make_async_copy(state.at[g], block.at[g], sems.at[g]) for g in range(fields)
     ]
     for copy in copies:
         copy.start()
-    for copy in copies:
-        copy.wait()
-
-
-def rims_kernel(state, rows, corner_a, corner_b):
-    fields, width = state.shape[:2]
-    even = is_even()
     row = iota((TILE, LANES), 0)
     outer = (row < REACH) | (row >= TILE - REACH)
-    for g in range(fields):
-        for pair in range(width // 2):
-            first = edge_tile(state, g, 2 * pair)
-            second = edge_tile(state, g, 2 * pair + 1)
-            rows[g, pair] = jnp.where(outer, first, pltpu.roll(second, TILE // 2, 0))
     near_a = jnp.where(even, width - 1, 0)
     near_b = jnp.where(even, 0, width - 1)
-    for corner, x in ((corner_a, near_a), (corner_b, near_b)):
-        for t in range(corner.shape[0]):
-            held = None
-            for k in range(SHARE):
-                g = t * SHARE + k
-                if g < fields:
-                    tile = edge_tile(state, g, x)
-                    if k:
-                        tile = jnp.where(corner_rows(k), pltpu.roll(tile, 2 * k, 0), held)
-                    held = tile
-            corner[t] = held
+    held = [None, None]
+    for g in range(fields):
+        copies[g].wait()
+        face_a[g] = block[g, pl.ds(jnp.where(even, last, 0), REACH)]
+        face_b[g] = block[g, pl.ds(jnp.where(even, 0, last), REACH)]
+        for pair in range(width // 2):
+            first = edge_tile(block, g, 2 * pair)
+            second = edge_tile(block, g, 2 * pair + 1)
+            rows[g, pair] = jnp.where(outer, first, pltpu.roll(second, TILE // 2, 0))
+        t, k = g // SHARE, g % SHARE
+        for n, (corner, x) in enumerate(((corner_a, near_a), (corner_b, near_b))):
+            tile = edge_tile(block, g, x)
+            if k:
+                tile = jnp.where(corner_rows(k), pltpu.roll(tile, 2 * k, 0), held[n])
+            held[n] = tile
+            if k == SHARE - 1 or g == fields - 1:
+                corner[t] = tile
 
 
 def bottom_mask(active):
@@ -146,10 +137,12 @@
 
 
 class Halo:
-    def __init__(self, merged, face_a, face_b, rest):
+    def __init__(self, merged, face_a, face_b, face_w, rest):
         count = 1 if merged else 2
         self.merged = merged
-        self.faces = (face_a, face_b)
+        self.faces = (face_a, face_b, face_w)
+        i = lax.axis_index("gx")
+        self.closing = (i == 0) | (i == lax.axis_size("gx") - 1)
         self.rows = rest[:count]
         self.corners = (rest[count : 2 * count], rest[2 * count : 3 * count])
         self.even = is_even()
@@ -161,7 +154,8 @@
         return jnp.where(upper, refs[0][index], refs[1][index])
 
     def face(self, g, side, n):
-        a, b = (ref[g, n] for ref in self.faces)
+        a, b, w = (ref[g, n] for ref in self.faces)
+        b = jnp.where(self.closing, w, b)
         return jnp.where(self.even, a, b) if side else jnp.where(self.even, b, a)
 
     def pair(self, g, n):
@@ -175,9 +169,9 @@
         return pltpu.roll(tile, TILE - 2 * k, 0) if k else tile
 
 
-def slab_kernel(merged, own, face_a, face_b, *rest):
+def slab_kernel(merged, own, face_a, face_b, face_w, *rest):
     slab = rest[-1]
-    halo = Halo(merged, face_a, face_b, rest[:-1])
+    halo = Halo(merged, face_a, face_b, face_w, rest[:-1])
     fields, height = own.shape[:2]
     width = 2 * halo.rows[0].shape[1]
     slot, _ = group_and_slot()
@@ -217,10 +211,10 @@
     return fresh
 
 
-def bulk_kernel(merged, state, zsum, mobility, shifts, face_a, face_b, *rest):
+def bulk_kernel(merged, state, zsum, mobility, shifts, face_a, face_b, face_w, *rest):
     done, lower, wide, first = rest[-10:-6]
     rims, sums, pending = rest[-6:-4], rest[-4:-2], rest[-2:]
-    halo = Halo(merged, face_a, face_b, rest[:-10])
+    halo = Halo(merged, face_a, face_b, face_w, rest[:-10])
     fields, width, height, length = state.shape
     grains = fields - 1
     rows = height + TILE
@@ -422,14 +416,14 @@
     merged = count_y == 2
     rows = height + TILE
     groups = -(-fields // SHARE)
-    block = shape(fields, width, height, length)
+    whole = shape(fields, width, height, length)
     packed = shape(fields, rows, length)
 
     def partner(i, kind):
         return (i + 1) % count_x if (i % 2 == 0) == (kind == 0) else (i - 1) % count_x
 
-    def swap(value, kind):
-        return lax.ppermute(value, "gx", [(i, partner(i, kind)) for i in range(count_x)])
+    def swap(value, pairs):
+        return lax.ppermute(value, "gx", pairs + [(j, i) for i, j in pairs])
 
     toward = [-1] if merged else [-1, 1]
 
@@ -447,46 +441,44 @@
             for d in toward
         ]
 
-    face_a, face_b = call(
-        faces_kernel,
-        [shape(fields, REACH, height, length)] * 2,
-        [state],
-        100000,
-        specs=[pl.BlockSpec(memory_space=pltpu.HBM)],
-        scratch=[pltpu.SemaphoreType.DMA((2,))],
-    )
-    got_b = swap(face_b, 1)
-    edge, corner_a, corner_b = call(
-        rims_kernel,
+    block, face_a, face_b, edge, corner_a, corner_b = call(
+        load_kernel,
         [
+            whole,
+            shape(fields, REACH, height, length),
+            shape(fields, REACH, height, length),
             shape(fields, width // 2, TILE, length),
             shape(groups, TILE, length),
             shape(groups, TILE, length),
         ],
-        [state],
+        [pltpu.with_memory_space_constraint(state, pltpu.HBM)],
         100000,
+        specs=[pl.BlockSpec(memory_space=pltpu.HBM)],
+        scratch=[pltpu.SemaphoreType.DMA((fields,))],
     )
+    got_w = swap(face_b, [(0, count_x - 1)])
     near = [
         lax.ppermute(edge, "gy", [(j, (j + d) % count_y) for j in range(count_y)])
         for d in toward
     ]
-    got_a = swap(face_a, 0)
+    got_a = swap(face_a, [(i, i + 1) for i in range(0, count_x, 2)])
+    got_b = swap(face_b, [(i, i + 1) for i in range(1, count_x - 1, 2)])
     far_b = diagonal(corner_b, 1)
     far_a = diagonal(corner_a, 0)
     zsum, own, marks = call(
         prepare_kernel,
-        [block, shape(fields, height, length), shape(rows, length)],
-        [state, seeds, frame_shifts],
+        [whole, shape(fields, height, length), shape(rows, length)],
+        [block, seeds, frame_shifts],
         5000000,
         specs=[VMEM, VMEM, SMEM],
     )
-    halo = [got_a, got_b, *near, *far_a, *far_b]
+    halo = [got_a, got_b, got_w, *near, *far_a, *far_b]
     slab = call(functools.partial(slab_kernel, merged), packed, [own, *halo], 100000)
     above = lax.ppermute(slab, "gz", [(k, k - 1) for k in range(1, count_z)])
     done, lower = call(
         functools.partial(bulk_kernel, merged),
-        [block, packed],
-        [state, zsum, mobility, frame_shifts, *halo],
+        [whole, packed],
+        [block, zsum, mobility, frame_shifts, *halo],
         20000000,
         specs=[VMEM, VMEM, SMEM, SMEM] + [VMEM] * len(halo),
         scratch=[
@@ -498,7 +490,7 @@
     )
     return call(
         crown_kernel,
-        block,
+        whole,
         [done, slab, above, lower, marks, mobility, frame_shifts],
         100000,
         specs=[VMEM] * 5 + [SMEM, SMEM],

time: 23.6 us -> 30.2 us (1.28)
  starting transfers between devices: 12 us -> 16.5 us
  waiting for transfers between devices: 2.85 us -> 4.89 us
  Pallas kernels: 7.1 us -> 8.42 us
  local copies, waits for them, and re-layouts: 1.38 us -> 0.11 us
    ppermute x2 -> x3, starting transfers between devices: 3.56 us -> 6.06 us  [swap(): return lax.ppermute(value, 'gx', pairs + [(j, i) for i, j in pairs])]
    ppermute x2, waiting for transfers between devices: 2.48 us -> 4.54 us  [diagonal(): lax.ppermute(value, ('gx', 'gy'), [(i * count_y + j, partner(i, kind) * c...]
    pallas_call x6 -> x5, Pallas kernels: 7.1 us -> 8.42 us  [call(): pl.pallas_call(kernel, out_shape=outs, in_specs=specs or [VMEM] * len(inp...]
    unnamed x11 -> x7, local copies, waits for them, and re-layouts: 1.38 us -> 0.11 us
    ppermute x1, starting transfers between devices: 4.12 us -> 5.36 us  [shards(): above = lax.ppermute(slab, 'gz', [(k, k - 1) for k in range(1, count_z)])]
    ppermute x2, starting transfers between devices: 2.2 us -> 2.93 us  [diagonal(): lax.ppermute(value, ('gx', 'gy'), [(i * count_y + j, partner(i, kind) * c...]
  transfers between devices with their start and end apart: 6 -> 7, of which waited for: 3 -> 3; matrix products, arithmetic and copies ran while one was open for 0% -> 0% of each run, Pallas kernels for 20% -> 16%
where the time goes in v2:
time: 30.2 us; the launch traced here: 30 us
  starting transfers between devices  16.5 us (55%)
  Pallas kernels  8.42 us (28%)
  waiting for transfers between devices  4.89 us (16%)
    pallas_call x5, Pallas kernels, call(): pl.pallas_call(kernel, out_shape=outs, in_specs=specs or [VMEM] * len(inp...  8.42 us
    ppermute x3, starting transfers between devices, swap(): return lax.ppermute(value, 'gx', pairs + [(j, i) for i, j in pairs])  6.06 us
    ppermute x1, starting transfers between devices, shards(): above = lax.ppermute(slab, 'gz', [(k, k - 1) for k in range(1, count_z)])  5.36 us
    ppermute x2, waiting for transfers between devices, diagonal(): lax.ppermute(value, ('gx', 'gy'), [(i * count_y + j, partner(i, kind) * c...  4.54 us
    ppermute x2, starting transfers between devices, diagonal(): lax.ppermute(value, ('gx', 'gy'), [(i * count_y + j, partner(i, kind) * c...  2.93 us
    ppermute x1, starting transfers between devices, shards(): lax.ppermute(edge, 'gy', [(j, (j + d) % count_y) for j in range(count_y)])  2.12 us
  transfers between devices with their start and end apart: 7, of which 3 were waited for; matrix products, arithmetic and copies ran while one was open for 0% of the time, Pallas kernels for 16%

profile of v2, /device:TPU:1, one launch (start us, length us, event | category | flops | bytes accessed | tf_op | source)
XLA Modules:
  0.0 30.0 jit_solution(17830802204313024687)
XLA Ops:
  0.0 0.0 copy-start.2
  0.0 0.0 copy-start
  0.0 1.4 %shard_map.46 = (f32[9,16,16,128]{3,2,1,0:T(8,128)S(1)}, f32[9,2,16,128]{3,2,1,0:T(8,128)S(1)}, f32[9,2,16,128]{3,2,1,0:T(8,128)S(1)}, f32[9,8,8,128]{3,2,1,0:T(...) custom-call(f32[9,16,16,128]{3,2,1,0:T(8,128)} %state.1), custom_call_target="tpu_custom_call" | custom-call | flops 100000 | bytes 100000 | tf_op jit(solution)/shard_map/pallas_call | solution.py:402
  1.4 2.1 %collective-permute-start.3 = (f32[9,8,8,128]{3,2,1,0:T(8,128)S(1)}, f32[9,8,8,128]{3,2,1,0:T(8,128)S(1)}, u32[]{:S(2)}, u32[]{:S(2)}) collective-permute-start(f32[9,8,8,128]{3,2,1,0:T(8,128)S(1)} %get-tuple-element.20), channel_id=1, source_target_pairs={{0,4},{4,0},{1,5},{5,1},{2,6},{6,2},{3,7},{7,3},{8,12},{12,8},{9,1... | collective-permute-start | bytes 884744 | tf_op jit(solution)/shard_map/ppermute | solution.py:461
  3.6 1.3 %collective-permute-start = (f32[9,2,16,128]{3,2,1,0:T(8,128)S(1)}, f32[9,2,16,128]{3,2,1,0:T(8,128)S(1)}, u32[]{:S(2)}, u32[]{:S(2)}) collective-permute-start(f32[9,2,16,128]{3,2,1,0:T(8,128)S(1)} %get-tuple-element.18), channel_id=1, source_target_pairs={{0,8},{16,24},{8,0},{24,16},{1,9},{17,25},{9,1},{25,17},{2,10},{18... | collective-permute-start | bytes 442376 | tf_op jit(solution)/shard_map/ppermute | solution.py:426
  4.9 4.1 %collective-permute-start.2 = (f32[9,2,16,128]{3,2,1,0:T(8,128)S(1)}, f32[9,2,16,128]{3,2,1,0:T(8,128)S(1)}, u32[]{:S(2)}, u32[]{:S(2)}) collective-permute-start(f32[9,2,16,128]{3,2,1,0:T(8,128)S(1)} %get-tuple-element.19), channel_id=1, source_target_pairs={{0,24},{24,0},{1,25},{25,1},{2,26},{26,2},{3,27},{27,3},{4,28},{28... | collective-permute-start | bytes 442376 | tf_op jit(solution)/shard_map/ppermute | solution.py:426
  9.0 0.7 %collective-permute-start.1 = (f32[9,2,16,128]{3,2,1,0:T(8,128)S(1)}, f32[9,2,16,128]{3,2,1,0:T(8,128)S(1)}, u32[]{:S(2)}, u32[]{:S(2)}) collective-permute-start(f32[9,2,16,128]{3,2,1,0:T(8,128)S(1)} %get-tuple-element.19), channel_id=1, source_target_pairs={{8,16},{16,8},{9,17},{17,9},{10,18},{18,10},{11,19},{19,11},{12,20... | collective-permute-start | bytes 442376 | tf_op jit(solution)/shard_map/ppermute | solution.py:426
  9.6 0.4 %collective-permute-start.4 = (f32[3,8,128]{2,1,0:T(8,128)S(1)}, f32[3,8,128]{2,1,0:T(8,128)S(1)}, u32[]{:S(2)}, u32[]{:S(2)}) collective-permute-start(f32[3,8,128]{2,1,0:T(8,128)S(1)} %get-tuple-element.21), channel_id=1, source_target_pairs={{0,12},{4,8},{8,4},{12,0},{16,28},{20,24},{24,20},{28,16},{1,13},{... | collective-permute-start | bytes 36872 | tf_op jit(solution)/shard_map/ppermute | solution.py:432
  10.0 3.5 %collective-permute-done.4.rest_1_ = f32[3,8,128]{2,1,0:T(8,128)S(1)} collective-permute-done((f32[3,8,128]{2,1,0:T(8,128)S(1)}, f32[3,8,128]{2,1,0:T(8,128)S(1)}, u32[]{:S(2)}, u32[]{:S(2)}) %collective-permute-start.4) | collective-permute-done | bytes 12320 | tf_op jit(solution)/shard_map/ppermute | solution.py:432
  13.5 2.5 %collective-permute-start.5 = (f32[3,8,128]{2,1,0:T(8,128)S(1)}, f32[3,8,128]{2,1,0:T(8,128)S(1)}, u32[]{:S(2)}, u32[]{:S(2)}) collective-permute-start(f32[3,8,128]{2,1,0:T(8,128)S(1)} %get-tuple-element.22), channel_id=1, source_target_pairs={{0,28},{4,24},{8,20},{12,16},{16,12},{20,8},{24,4},{28,0},{1,29},{... | collective-permute-start | bytes 36872 | tf_op jit(solution)/shard_map/ppermute | solution.py:432
  16.0 0.0 copy-done.2
  16.0 0.1 copy.5.seeds
  16.1 0.0 copy-start.1
  16.2 0.0 copy-done
  16.2 1.5 %shard_map.47 = (f32[9,16,16,128]{3,2,1,0:T(8,128)S(1)}, f32[9,16,128]{2,1,0:T(8,128)S(1)}, f32[24,128]{1,0:T(8,128)S(1)}) custom-call(f32[9,16,16,128]{3,2,1,0:T(8,128)S(1)} %get-tuple-element.16.state, s32[2,2,64,32]{3,2,1,0:T(8,128)S(1)} %copy.5.seeds, s32[2]{0:T(128)S(1)} %copy-done), custom_call_target="tpu_custom_call" | custom-call | flops 5000000 | bytes 5000000 | tf_op jit(solution)/shard_map/pallas_call | solution.py:402
  17.7 1.1 %collective-permute-done.5.rest_2_ = f32[3,8,128]{2,1,0:T(8,128)S(1)} collective-permute-done((f32[3,8,128]{2,1,0:T(8,128)S(1)}, f32[3,8,128]{2,1,0:T(8,128)S(1)}, u32[]{:S(2)}, u32[]{:S(2)}) %collective-permute-start.5) | collective-permute-done | bytes 12320 | tf_op jit(solution)/shard_map/ppermute | solution.py:432
  18.8 0.0 collective-permute-done.face_a
  18.8 0.0 collective-permute-done.2.face_w
  18.8 0.0 collective-permute-done.1.face_b
  18.8 0.0 collective-permute-done.3.rest_0_
  18.8 0.3 %shard_map.49.slab = f32[9,24,128]{2,1,0:T(8,128)S(1)} custom-call(f32[9,16,128]{2,1,0:T(8,128)S(1)} %get-tuple-element.24.own, f32[9,2,16,128]{3,2,1,0:T(8,128)S(1)} %collective-permute-done.face_a, f32[9,2,16,128]{3,2,1,0:T(8,128)S(1)} %collective-permute-done.1.face_b, f32[9,2,16,128]{3,2,1,0:T(8,128)S(1)} %collective-permute-done.2.face_w, ...), custom_call_target="tpu_custom_call" | custom-call | flops 100000 | bytes 100000 | tf_op jit(solution)/shard_map/pallas_call | solution.py:402
  19.1 5.4 %collective-permute-start.6 = (f32[9,24,128]{2,1,0:T(8,128)S(1)}, f32[9,24,128]{2,1,0:T(8,128)S(1)}, u32[]{:S(2)}, u32[]{:S(2)}) collective-permute-start(f32[9,24,128]{2,1,0:T(8,128)S(1)} %shard_map.49.slab), channel_id=1, source_target_pairs={{1,0},{2,1},{3,2},{5,4},{6,5},{7,6},{9,8},{10,9},{11,10},{13,12},{... | collective-permute-start | bytes 331784 | tf_op jit(solution)/shard_map/ppermute | solution.py:477
  24.5 0.0 copy-done.1
  24.5 3.2 %shard_map.48 = (f32[9,16,16,128]{3,2,1,0:T(8,128)S(1)}, f32[9,24,128]{2,1,0:T(8,128)S(1)}) custom-call(f32[9,16,16,128]{3,2,1,0:T(8,128)S(1)} %get-tuple-element.16.state, f32[9,16,16,128]{3,2,1,0:T(8,128)S(1)} %get-tuple-element.17.zsum, f32[8]{0:T(128)S(1)} %copy-done.1, s32[2]{0:T(128)S(1)} %copy-done, ...), custom_call_target="tpu_custom_call" | custom-call | flops 20000000 | bytes 20000000 | tf_op jit(solution)/shard_map/pallas_call | solution.py:402
  27.6 0.3 %collective-permute-done.6.above = f32[9,24,128]{2,1,0:T(8,128)S(1)} collective-permute-done((f32[9,24,128]{2,1,0:T(8,128)S(1)}, f32[9,24,128]{2,1,0:T(8,128)S(1)}, u32[]{:S(2)}, u32[]{:S(2)}) %collective-permute-start.6) | collective-permute-done | bytes 110624 | tf_op jit(solution)/shard_map/ppermute | solution.py:477
  28.0 2.0 %shard_map.50 = f32[9,16,16,128]{3,2,1,0:T(8,128)} custom-call(f32[9,16,16,128]{3,2,1,0:T(8,128)S(1)} %get-tuple-element.23.done, f32[9,24,128]{2,1,0:T(8,128)S(1)} %shard_map.49.slab, f32[9,24,128]{2,1,0:T(8,128)S(1)} %collective-permute-done.6.above, f32[9,24,128]{2,1,0:T(8,128)S(1)} %get-tuple-element.25.lower, f32[24,128]{1,0:T(8,128)S(1)} %get-tuple-element.26.marks, ...), custom_call_target="tpu_custom_call" | custom-call | flops 100000 | bytes 100000 | tf_op jit(solution)/shard_map/pallas_call | solution.py:402
Async XLA Ops:
  0.0 16.0 %copy-start.2 = (s32[2,2,64,32]{2,3,1,0:T(8,128)S(1)}, s32[2,2,64,32]{2,3,1,0:T(8,128)}, u32[]{:S(2)}) copy-start(s32[2,2,64,32]{2,3,1,0:T(8,128)} %param.6) | copy-start | bytes 98308
  0.0 16.2 %copy-start = (s32[2]{0:T(128)S(1)}, s32[2]{0:T(128)}, u32[]{:S(2)}) copy-start(s32[2]{0:T(128)} %shifts.5) | copy-start | bytes 28
  1.4 17.3 %collective-permute-start.3 = (f32[9,8,8,128]{3,2,1,0:T(8,128)S(1)}, f32[9,8,8,128]{3,2,1,0:T(8,128)S(1)}, u32[]{:S(2)}, u32[]{:S(2)}) collective-permute-start(f32[9,8,8,128]{3,2,1,0:T(8,128)S(1)} %get-tuple-element.20), channel_id=1, source_target_pairs={{0,4},{4,0},{1,5},{5,1},{2,6},{6,2},{3,7},{7,3},{8,12},{12,8},{9,1... | collective-permute-start | bytes 884744 | tf_op jit(solution)/shard_map/ppermute | solution.py:461
  3.6 15.2 %collective-permute-start = (f32[9,2,16,128]{3,2,1,0:T(8,128)S(1)}, f32[9,2,16,128]{3,2,1,0:T(8,128)S(1)}, u32[]{:S(2)}, u32[]{:S(2)}) collective-permute-start(f32[9,2,16,128]{3,2,1,0:T(8,128)S(1)} %get-tuple-element.18), channel_id=1, source_target_pairs={{0,8},{16,24},{8,0},{24,16},{1,9},{17,25},{9,1},{25,17},{2,10},{18... | collective-permute-start | bytes 442376 | tf_op jit(solution)/shard_map/ppermute | solution.py:426
  4.9 13.9 %collective-permute-start.2 = (f32[9,2,16,128]{3,2,1,0:T(8,128)S(1)}, f32[9,2,16,128]{3,2,1,0:T(8,128)S(1)}, u32[]{:S(2)}, u32[]{:S(2)}) collective-permute-start(f32[9,2,16,128]{3,2,1,0:T(8,128)S(1)} %get-tuple-element.19), channel_id=1, source_target_pairs={{0,24},{24,0},{1,25},{25,1},{2,26},{26,2},{3,27},{27,3},{4,28},{28... | collective-permute-start | bytes 442376 | tf_op jit(solution)/shard_map/ppermute | solution.py:426
  9.0 9.8 %collective-permute-start.1 = (f32[9,2,16,128]{3,2,1,0:T(8,128)S(1)}, f32[9,2,16,128]{3,2,1,0:T(8,128)S(1)}, u32[]{:S(2)}, u32[]{:S(2)}) collective-permute-start(f32[9,2,16,128]{3,2,1,0:T(8,128)S(1)} %get-tuple-element.19), channel_id=1, source_target_pairs={{8,16},{16,8},{9,17},{17,9},{10,18},{18,10},{11,19},{19,11},{12,20... | collective-permute-start | bytes 442376 | tf_op jit(solution)/shard_map/ppermute | solution.py:426
  9.6 3.9 %collective-permute-start.4 = (f32[3,8,128]{2,1,0:T(8,128)S(1)}, f32[3,8,128]{2,1,0:T(8,128)S(1)}, u32[]{:S(2)}, u32[]{:S(2)}) collective-permute-start(f32[3,8,128]{2,1,0:T(8,128)S(1)} %get-tuple-element.21), channel_id=1, source_target_pairs={{0,12},{4,8},{8,4},{12,0},{16,28},{20,24},{24,20},{28,16},{1,13},{... | collective-permute-start | bytes 36872 | tf_op jit(solution)/shard_map/ppermute | solution.py:432
  13.5 5.2 %collective-permute-start.5 = (f32[3,8,128]{2,1,0:T(8,128)S(1)}, f32[3,8,128]{2,1,0:T(8,128)S(1)}, u32[]{:S(2)}, u32[]{:S(2)}) collective-permute-start(f32[3,8,128]{2,1,0:T(8,128)S(1)} %get-tuple-element.22), channel_id=1, source_target_pairs={{0,28},{4,24},{8,20},{12,16},{16,12},{20,8},{24,4},{28,0},{1,29},{... | collective-permute-start | bytes 36872 | tf_op jit(solution)/shard_map/ppermute | solution.py:432
  16.1 8.3 %copy-start.1 = (f32[8]{0:T(128)S(1)}, f32[8]{0:T(128)}, u32[]{:S(2)}) copy-start(f32[8]{0:T(128)} %mobility.3) | copy-start | bytes 100
  19.1 8.9 %collective-permute-start.6 = (f32[9,24,128]{2,1,0:T(8,128)S(1)}, f32[9,24,128]{2,1,0:T(8,128)S(1)}, u32[]{:S(2)}, u32[]{:S(2)}) collective-permute-start(f32[9,24,128]{2,1,0:T(8,128)S(1)} %shard_map.49.slab), channel_id=1, source_target_pairs={{1,0},{2,1},{3,2},{5,4},{6,5},{7,6},{9,8},{10,9},{11,10},{13,12},{... | collective-permute-start | bytes 331784 | tf_op jit(solution)/shard_map/ppermute | solution.py:477

commit v3 on v2

--- a/solution.py
+++ b/solution.py
@@ -35,8 +35,8 @@
     return lax.rem(lax.axis_index("gx"), 2) == 0
 
 
-def group_and_slot():
-    lane = iota((1, LANES), 1)
+def group_and_slot(ahead=0):
+    lane = iota((1, LANES), 1) + ahead
     slot = lax.shift_right_logical(lane * 43, 8)
     return slot, lane - slot * GROUP
 
@@ -53,7 +53,14 @@
     return (row == 2 * k) | (row == (2 * k + TILE - 1) % TILE)
 
 
-def load_kernel(state, block, face_a, face_b, rows, corner_a, corner_b, sems):
+def outer_face_kernel(state, face, sem):
+    start = jnp.where(is_even(), 0, state.shape[1] - REACH)
+    copy = pltpu.make_async_copy(state.at[:, pl.ds(start, REACH)], face, sem)
+    copy.start()
+    copy.wait()
+
+
+def load_kernel(state, block, face_a, rows, corner_a, corner_b, sems):
     fields, width = state.shape[:2]
     even = is_even()
     last = width - REACH
@@ -70,7 +77,6 @@
     for g in range(fields):
         copies[g].wait()
         face_a[g] = block[g, pl.ds(jnp.where(even, last, 0), REACH)]
-        face_b[g] = block[g, pl.ds(jnp.where(even, 0, last), REACH)]
         for pair in range(width // 2):
             first = edge_tile(block, g, 2 * pair)
             second = edge_tile(block, g, 2 * pair + 1)
@@ -137,12 +143,10 @@
 
 
 class Halo:
-    def __init__(self, merged, face_a, face_b, face_w, rest):
+    def __init__(self, merged, face_a, face_b, rest):
         count = 1 if merged else 2
         self.merged = merged
-        self.faces = (face_a, face_b, face_w)
-        i = lax.axis_index("gx")
-        self.closing = (i == 0) | (i == lax.axis_size("gx") - 1)
+        self.faces = (face_a, face_b)
         self.rows = rest[:count]
         self.corners = (rest[count : 2 * count], rest[2 * count : 3 * count])
         self.even = is_even()
@@ -154,8 +158,7 @@
         return jnp.where(upper, refs[0][index], refs[1][index])
 
     def face(self, g, side, n):
-        a, b, w = (ref[g, n] for ref in self.faces)
-        b = jnp.where(self.closing, w, b)
+        a, b = (ref[g, n] for ref in self.faces)
         return jnp.where(self.even, a, b) if side else jnp.where(self.even, b, a)
 
     def pair(self, g, n):
@@ -169,9 +172,9 @@
         return pltpu.roll(tile, TILE - 2 * k, 0) if k else tile
 
 
-def slab_kernel(merged, own, face_a, face_b, face_w, *rest):
+def slab_kernel(merged, own, face_a, face_b, *rest):
     slab = rest[-1]
-    halo = Halo(merged, face_a, face_b, face_w, rest[:-1])
+    halo = Halo(merged, face_a, face_b, rest[:-1])
     fields, height = own.shape[:2]
     width = 2 * halo.rows[0].shape[1]
     slot, _ = group_and_slot()
@@ -211,10 +214,10 @@
     return fresh
 
 
-def bulk_kernel(merged, state, zsum, mobility, shifts, face_a, face_b, face_w, *rest):
+def bulk_kernel(merged, state, zsum, mobility, shifts, face_a, face_b, *rest):
     done, lower, wide, first = rest[-10:-6]
     rims, sums, pending = rest[-6:-4], rest[-4:-2], rest[-2:]
-    halo = Halo(merged, face_a, face_b, face_w, rest[:-10])
+    halo = Halo(merged, face_a, face_b, rest[:-10])
     fields, width, height, length = state.shape
     grains = fields - 1
     rows = height + TILE
@@ -222,7 +225,7 @@
     span = float(length * lax.axis_size("gz"))
     base = lax.axis_index("gz") * length
     lane = iota((1, LANES), 1)
-    slot_of, _ = group_and_slot()
+    slot_of, _ = group_and_slot(1)
     speeds = [mobility[g] for g in range(grains)]
     own = slice(TILE, TILE + height)
 
@@ -276,7 +279,7 @@
     def put_lower(slot, source):
         for g in range(fields):
             moved = pltpu.roll(source(g), slot, 1)
-            lower[g] = jnp.where(slot_of * GROUP + REACH + 1 == slot, moved, lower[g])
+            lower[g] = jnp.where(slot_of * GROUP + REACH == slot, moved, lower[g])
 
     lower[...] = jnp.zeros_like(lower)
     for x in (1, width + REACH):
@@ -296,13 +299,13 @@
         for part in range(UNROLL):
             x = block * UNROLL + part
             now, after = rims[part % 2], rims[1 - part % 2]
-            put_lower((x + 1) * GROUP + REACH + 1, plane_of(x))
+            put_lower((x + 1) * GROUP + REACH, plane_of(x))
             plane_first(x + REACH, lambda g: zsum[g, x], lambda g: now[g])
             for g in range(fields):
                 after[g] = along(wide[g, x + REACH + 1, 0:TILE], mask_first)
 
     for x in (width, width + 1):
-        put_lower((x + 1) * GROUP + REACH + 1, plane_of(x))
+        put_lower((x + 1) * GROUP + REACH, plane_of(x))
 
     theta_second = theta_of(REACH)
     mask_second = bottom_mask(lax.axis_index("gz") == 0)
@@ -351,6 +354,7 @@
             return jnp.full((rows, LANES), melt_solute, jnp.float32)
         return jnp.where(marks[...] == float(g), nucleus, 0.0)
 
+    below = (place == 0) | (place == GROUP - 1)
     planted = (place >= REACH) & (place < 2 * REACH)
     zero = jnp.zeros((rows, LANES), jnp.float32)
 
@@ -377,15 +381,15 @@
         value = middle[g]
         value = jnp.where(topmost & jnp.logical_not(early) & planted, entering(g), value)
         value = jnp.where(topmost & (place >= 2 * REACH), 0.0, value)
-        after.append(jnp.where(place < REACH, lower[g], pltpu.roll(value, 1, 1)))
-    final = advance(after, theta_of(REACH + 1 + REACH))
+        after.append(jnp.where(below, lower[g], value))
+    final = advance(after, theta_of(REACH + REACH))
 
     top = iota((1, LANES), 1) >= LANES - 2 * REACH
     copies = []
     for g in range(fields):
         cut = final[g][0:height]
         for x in range(width):
-            shift = (LANES - 2 * REACH - (x + REACH) * GROUP - 1) % LANES
+            shift = (LANES - 2 * REACH - (x + REACH) * GROUP) % LANES
             whole[g, x] = jnp.where(top, pltpu.roll(cut, shift, 1), done[g, x])
         copy = pltpu.make_async_copy(whole.at[g], out.at[g], sems.at[g])
         copy.start()
@@ -441,28 +445,37 @@
             for d in toward
         ]
 
-    block, face_a, face_b, edge, corner_a, corner_b = call(
+    held = pltpu.with_memory_space_constraint(state, pltpu.HBM)
+    in_hbm = [pl.BlockSpec(memory_space=pltpu.HBM)]
+    face = shape(fields, REACH, height, length)
+    face_b = call(
+        outer_face_kernel,
+        face,
+        [held],
+        100000,
+        specs=in_hbm,
+        scratch=[pltpu.SemaphoreType.DMA(())],
+    )
+    got_b = swap(face_b, [(i, (i + 1) % count_x) for i in range(1, count_x, 2)])
+    block, face_a, edge, corner_a, corner_b = call(
         load_kernel,
         [
             whole,
-            shape(fields, REACH, height, length),
-            shape(fields, REACH, height, length),
+            face,
             shape(fields, width // 2, TILE, length),
             shape(groups, TILE, length),
             shape(groups, TILE, length),
         ],
-        [pltpu.with_memory_space_constraint(state, pltpu.HBM)],
+        [held],
         100000,
-        specs=[pl.BlockSpec(memory_space=pltpu.HBM)],
+        specs=in_hbm,
         scratch=[pltpu.SemaphoreType.DMA((fields,))],
     )
-    got_w = swap(face_b, [(0, count_x - 1)])
     near = [
         lax.ppermute(edge, "gy", [(j, (j + d) % count_y) for j in range(count_y)])
         for d in toward
     ]
     got_a = swap(face_a, [(i, i + 1) for i in range(0, count_x, 2)])
-    got_b = swap(face_b, [(i, i + 1) for i in range(1, count_x - 1, 2)])
     far_b = diagonal(corner_b, 1)
     far_a = diagonal(corner_a, 0)
     zsum, own, marks = call(
@@ -472,7 +485,7 @@
         5000000,
         specs=[VMEM, VMEM, SMEM],
     )
-    halo = [got_a, got_b, got_w, *near, *far_a, *far_b]
+    halo = [got_a, got_b, *near, *far_a, *far_b]
     slab = call(functools.partial(slab_kernel, merged), packed, [own, *halo], 100000)
     above = lax.ppermute(slab, "gz", [(k, k - 1) for k in range(1, count_z)])
     done, lower = call(

time: 30.2 us -> 25.3 us (0.84)
  starting transfers between devices: 16.5 us -> 12.2 us
  waiting for transfers between devices: 4.89 us -> 3.54 us
  Pallas kernels: 8.42 us -> 9.25 us
    ppermute x3 -> x2, starting transfers between devices: 6.06 us -> 3.39 us  [swap(): return lax.ppermute(value, 'gx', pairs + [(j, i) for i, j in pairs])]
    ppermute x2, waiting for transfers between devices: 4.54 us -> 3.17 us  [diagonal(): lax.ppermute(value, ('gx', 'gy'), [(i * count_y + j, partner(i, kind) * c...]
    ppermute x1, starting transfers between devices: 5.36 us -> 4.25 us  [shards(): above = lax.ppermute(slab, 'gz', [(k, k - 1) for k in range(1, count_z)])]
    pallas_call x5 -> x6, Pallas kernels: 8.42 us -> 9.25 us  [call(): pl.pallas_call(kernel, out_shape=outs, in_specs=specs or [VMEM] * len(inp...]
    ppermute x2, starting transfers between devices: 2.93 us -> 2.44 us  [diagonal(): lax.ppermute(value, ('gx', 'gy'), [(i * count_y + j, partner(i, kind) * c...]
  transfers between devices with their start and end apart: 7 -> 6, of which waited for: 3 -> 2; matrix products, arithmetic and copies ran while one was open for 0% -> 0% of each run, Pallas kernels for 16% -> 22%
where the time goes in v3:
time: 25.3 us; the launch traced here: 25.2 us
  starting transfers between devices  12.2 us (48%)
  Pallas kernels  9.25 us (37%)
  waiting for transfers between devices  3.54 us (14%)
    pallas_call x6, Pallas kernels, call(): pl.pallas_call(kernel, out_shape=outs, in_specs=specs or [VMEM] * len(inp...  9.25 us
    ppermute x1, starting transfers between devices, shards(): above = lax.ppermute(slab, 'gz', [(k, k - 1) for k in range(1, count_z)])  4.25 us
    ppermute x2, starting transfers between devices, swap(): return lax.ppermute(value, 'gx', pairs + [(j, i) for i, j in pairs])  3.39 us
    ppermute x2, waiting for transfers between devices, diagonal(): lax.ppermute(value, ('gx', 'gy'), [(i * count_y + j, partner(i, kind) * c...  3.17 us
    ppermute x2, starting transfers between devices, diagonal(): lax.ppermute(value, ('gx', 'gy'), [(i * count_y + j, partner(i, kind) * c...  2.44 us
    ppermute x1, starting transfers between devices, shards(): lax.ppermute(edge, 'gy', [(j, (j + d) % count_y) for j in range(count_y)])  2.12 us
  transfers between devices with their start and end apart: 6, of which 2 were waited for; matrix products, arithmetic and copies ran while one was open for 0% of the time, Pallas kernels for 22%

profile of v3, /device:TPU:1, one launch (start us, length us, event | category | flops | bytes accessed | tf_op | source)
XLA Modules:
  0.0 25.2 jit_solution(9617050372097614026)
XLA Ops:
  0.0 0.0 copy-start.2
  0.0 0.0 copy-start
  0.0 1.4 %shard_map.46 = (f32[9,16,16,128]{3,2,1,0:T(8,128)S(1)}, f32[9,2,16,128]{3,2,1,0:T(8,128)S(1)}, f32[9,8,8,128]{3,2,1,0:T(8,128)S(1)}, f32[3,8,128]{2,1,0:T(8,128)S(1)}, f32[3,8,128]{2,1,0:T(8,128)S(1)}) custom-call(f32[9,16,16,128]{3,2,1,0:T(8,128)} %state.3), custom_call_target="tpu_custom_call" | custom-call | flops 100000 | bytes 100000 | tf_op jit(solution)/shard_map/pallas_call | solution.py:406
  1.4 2.1 %collective-permute-start.2 = (f32[9,8,8,128]{3,2,1,0:T(8,128)S(1)}, f32[9,8,8,128]{3,2,1,0:T(8,128)S(1)}, u32[]{:S(2)}, u32[]{:S(2)}) collective-permute-start(f32[9,8,8,128]{3,2,1,0:T(8,128)S(1)} %get-tuple-element.18), channel_id=1, source_target_pairs={{0,4},{4,0},{1,5},{5,1},{2,6},{6,2},{3,7},{7,3},{8,12},{12,8},{9,1... | collective-permute-start | bytes 884744 | tf_op jit(solution)/shard_map/ppermute | solution.py:475
  3.6 0.9 %shard_map.48 = f32[9,2,16,128]{3,2,1,0:T(8,128)S(1)} custom-call(f32[9,16,16,128]{3,2,1,0:T(8,128)} %state.3), custom_call_target="tpu_custom_call" | custom-call | flops 100000 | bytes 100000 | tf_op jit(solution)/shard_map/pallas_call | solution.py:406
  4.5 0.0 copy-start.1
  4.5 3.4 %collective-permute-start.1 = (f32[9,2,16,128]{3,2,1,0:T(8,128)S(1)}, f32[9,2,16,128]{3,2,1,0:T(8,128)S(1)}, u32[]{:S(2)}, u32[]{:S(2)}) collective-permute-start(f32[9,2,16,128]{3,2,1,0:T(8,128)S(1)} %shard_map.48), channel_id=1, source_target_pairs={{8,16},{24,0},{16,8},{0,24},{9,17},{25,1},{17,9},{1,25},{10,18},{2... | collective-permute-start | bytes 442376 | tf_op jit(solution)/shard_map/ppermute | solution.py:430
  7.9 0.0 collective-permute-start
  7.9 1.4 %collective-permute-start.3 = (f32[3,8,128]{2,1,0:T(8,128)S(1)}, f32[3,8,128]{2,1,0:T(8,128)S(1)}, u32[]{:S(2)}, u32[]{:S(2)}) collective-permute-start(f32[3,8,128]{2,1,0:T(8,128)S(1)} %get-tuple-element.19), channel_id=1, source_target_pairs={{0,12},{4,8},{8,4},{12,0},{16,28},{20,24},{24,20},{28,16},{1,13},{... | collective-permute-start | bytes 36872 | tf_op jit(solution)/shard_map/ppermute | solution.py:436
  9.3 1.0 %collective-permute-start.4 = (f32[3,8,128]{2,1,0:T(8,128)S(1)}, f32[3,8,128]{2,1,0:T(8,128)S(1)}, u32[]{:S(2)}, u32[]{:S(2)}) collective-permute-start(f32[3,8,128]{2,1,0:T(8,128)S(1)} %get-tuple-element.20), channel_id=1, source_target_pairs={{0,28},{4,24},{8,20},{12,16},{16,12},{20,8},{24,4},{28,0},{1,29},{... | collective-permute-start | bytes 36872 | tf_op jit(solution)/shard_map/ppermute | solution.py:436
  10.3 0.0 copy-done.2
  10.3 0.1 copy.5.seeds
  10.4 0.0 copy-done
  10.5 1.5 %shard_map.47 = (f32[9,16,16,128]{3,2,1,0:T(8,128)S(1)}, f32[9,16,128]{2,1,0:T(8,128)S(1)}, f32[24,128]{1,0:T(8,128)S(1)}) custom-call(f32[9,16,16,128]{3,2,1,0:T(8,128)S(1)} %get-tuple-element.15.state, s32[2,2,64,32]{3,2,1,0:T(8,128)S(1)} %copy.5.seeds, s32[2]{0:T(128)S(1)} %copy-done), custom_call_target="tpu_custom_call" | custom-call | flops 5000000 | bytes 5000000 | tf_op jit(solution)/shard_map/pallas_call | solution.py:406
  12.0 3.2 %collective-permute-done.3.rest_1_ = f32[3,8,128]{2,1,0:T(8,128)S(1)} collective-permute-done((f32[3,8,128]{2,1,0:T(8,128)S(1)}, f32[3,8,128]{2,1,0:T(8,128)S(1)}, u32[]{:S(2)}, u32[]{:S(2)}) %collective-permute-start.3) | collective-permute-done | bytes 12320 | tf_op jit(solution)/shard_map/ppermute | solution.py:436
  15.1 0.0 collective-permute-done.4.rest_2_
  15.1 0.0 collective-permute-done.1.face_b
  15.1 0.0 collective-permute-done.face_a
  15.2 0.0 collective-permute-done.2.rest_0_
  15.2 0.3 %shard_map.50.slab = f32[9,24,128]{2,1,0:T(8,128)S(1)} custom-call(f32[9,16,128]{2,1,0:T(8,128)S(1)} %get-tuple-element.22.own, f32[9,2,16,128]{3,2,1,0:T(8,128)S(1)} %collective-permute-done.face_a, f32[9,2,16,128]{3,2,1,0:T(8,128)S(1)} %collective-permute-done.1.face_b, f32[9,8,8,128]{3,2,1,0:T(8,128)S(1)} %collective-permute-done.2.rest_0_, ...), custom_call_target="tpu_custom_call" | custom-call | flops 100000 | bytes 100000 | tf_op jit(solution)/shard_map/pallas_call | solution.py:406
  15.5 4.2 %collective-permute-start.5 = (f32[9,24,128]{2,1,0:T(8,128)S(1)}, f32[9,24,128]{2,1,0:T(8,128)S(1)}, u32[]{:S(2)}, u32[]{:S(2)}) collective-permute-start(f32[9,24,128]{2,1,0:T(8,128)S(1)} %shard_map.50.slab), channel_id=1, source_target_pairs={{1,0},{2,1},{3,2},{5,4},{6,5},{7,6},{9,8},{10,9},{11,10},{13,12},{... | collective-permute-start | bytes 331784 | tf_op jit(solution)/shard_map/ppermute | solution.py:490
  19.7 0.0 copy-done.1
  19.7 3.1 %shard_map.49 = (f32[9,16,16,128]{3,2,1,0:T(8,128)S(1)}, f32[9,24,128]{2,1,0:T(8,128)S(1)}) custom-call(f32[9,16,16,128]{3,2,1,0:T(8,128)S(1)} %get-tuple-element.15.state, f32[9,16,16,128]{3,2,1,0:T(8,128)S(1)} %get-tuple-element.16.zsum, f32[8]{0:T(128)S(1)} %copy-done.1, s32[2]{0:T(128)S(1)} %copy-done, ...), custom_call_target="tpu_custom_call" | custom-call | flops 20000000 | bytes 20000000 | tf_op jit(solution)/shard_map/pallas_call | solution.py:406
  22.9 0.4 %collective-permute-done.5.above = f32[9,24,128]{2,1,0:T(8,128)S(1)} collective-permute-done((f32[9,24,128]{2,1,0:T(8,128)S(1)}, f32[9,24,128]{2,1,0:T(8,128)S(1)}, u32[]{:S(2)}, u32[]{:S(2)}) %collective-permute-start.5) | collective-permute-done | bytes 110624 | tf_op jit(solution)/shard_map/ppermute | solution.py:490
  23.3 1.9 %shard_map.51 = f32[9,16,16,128]{3,2,1,0:T(8,128)} custom-call(f32[9,16,16,128]{3,2,1,0:T(8,128)S(1)} %get-tuple-element.21.done, f32[9,24,128]{2,1,0:T(8,128)S(1)} %shard_map.50.slab, f32[9,24,128]{2,1,0:T(8,128)S(1)} %collective-permute-done.5.above, f32[9,24,128]{2,1,0:T(8,128)S(1)} %get-tuple-element.23.lower, f32[24,128]{1,0:T(8,128)S(1)} %get-tuple-element.24.marks, ...), custom_call_target="tpu_custom_call" | custom-call | flops 100000 | bytes 100000 | tf_op jit(solution)/shard_map/pallas_call | solution.py:406
Async XLA Ops:
  0.0 10.3 %copy-start.2 = (s32[2,2,64,32]{2,3,1,0:T(8,128)S(1)}, s32[2,2,64,32]{2,3,1,0:T(8,128)}, u32[]{:S(2)}) copy-start(s32[2,2,64,32]{2,3,1,0:T(8,128)} %param.6) | copy-start | bytes 98308
  0.0 10.4 %copy-start = (s32[2]{0:T(128)S(1)}, s32[2]{0:T(128)}, u32[]{:S(2)}) copy-start(s32[2]{0:T(128)} %shifts.5) | copy-start | bytes 28
  1.4 13.7 %collective-permute-start.2 = (f32[9,8,8,128]{3,2,1,0:T(8,128)S(1)}, f32[9,8,8,128]{3,2,1,0:T(8,128)S(1)}, u32[]{:S(2)}, u32[]{:S(2)}) collective-permute-start(f32[9,8,8,128]{3,2,1,0:T(8,128)S(1)} %get-tuple-element.18), channel_id=1, source_target_pairs={{0,4},{4,0},{1,5},{5,1},{2,6},{6,2},{3,7},{7,3},{8,12},{12,8},{9,1... | collective-permute-start | bytes 884744 | tf_op jit(solution)/shard_map/ppermute | solution.py:475
  4.5 15.2 %copy-start.1 = (f32[8]{0:T(128)S(1)}, f32[8]{0:T(128)}, u32[]{:S(2)}) copy-start(f32[8]{0:T(128)} %mobility.3) | copy-start | bytes 100
  4.5 10.6 %collective-permute-start.1 = (f32[9,2,16,128]{3,2,1,0:T(8,128)S(1)}, f32[9,2,16,128]{3,2,1,0:T(8,128)S(1)}, u32[]{:S(2)}, u32[]{:S(2)}) collective-permute-start(f32[9,2,16,128]{3,2,1,0:T(8,128)S(1)} %shard_map.48), channel_id=1, source_target_pairs={{8,16},{24,0},{16,8},{0,24},{9,17},{25,1},{17,9},{1,25},{10,18},{2... | collective-permute-start | bytes 442376 | tf_op jit(solution)/shard_map/ppermute | solution.py:430
  7.9 7.3 %collective-permute-start = (f32[9,2,16,128]{3,2,1,0:T(8,128)S(1)}, f32[9,2,16,128]{3,2,1,0:T(8,128)S(1)}, u32[]{:S(2)}, u32[]{:S(2)}) collective-permute-start(f32[9,2,16,128]{3,2,1,0:T(8,128)S(1)} %get-tuple-element.17), channel_id=1, source_target_pairs={{0,8},{16,24},{8,0},{24,16},{1,9},{17,25},{9,1},{25,17},{2,10},{18... | collective-permute-start | bytes 442376 | tf_op jit(solution)/shard_map/ppermute | solution.py:430
  7.9 7.2 %collective-permute-start.3 = (f32[3,8,128]{2,1,0:T(8,128)S(1)}, f32[3,8,128]{2,1,0:T(8,128)S(1)}, u32[]{:S(2)}, u32[]{:S(2)}) collective-permute-start(f32[3,8,128]{2,1,0:T(8,128)S(1)} %get-tuple-element.19), channel_id=1, source_target_pairs={{0,12},{4,8},{8,4},{12,0},{16,28},{20,24},{24,20},{28,16},{1,13},{... | collective-permute-start | bytes 36872 | tf_op jit(solution)/shard_map/ppermute | solution.py:436
  9.3 5.8 %collective-permute-start.4 = (f32[3,8,128]{2,1,0:T(8,128)S(1)}, f32[3,8,128]{2,1,0:T(8,128)S(1)}, u32[]{:S(2)}, u32[]{:S(2)}) collective-permute-start(f32[3,8,128]{2,1,0:T(8,128)S(1)} %get-tuple-element.20), channel_id=1, source_target_pairs={{0,28},{4,24},{8,20},{12,16},{16,12},{20,8},{24,4},{28,0},{1,29},{... | collective-permute-start | bytes 36872 | tf_op jit(solution)/shard_map/ppermute | solution.py:436
  15.5 7.8 %collective-permute-start.5 = (f32[9,24,128]{2,1,0:T(8,128)S(1)}, f32[9,24,128]{2,1,0:T(8,128)S(1)}, u32[]{:S(2)}, u32[]{:S(2)}) collective-permute-start(f32[9,24,128]{2,1,0:T(8,128)S(1)} %shard_map.50.slab), channel_id=1, source_target_pairs={{1,0},{2,1},{3,2},{5,4},{6,5},{7,6},{9,8},{10,9},{11,10},{13,12},{... | collective-permute-start | bytes 331784 | tf_op jit(solution)/shard_map/ppermute | solution.py:490

commit v4 on v3

--- a/solution.py
+++ b/solution.py
@@ -1,4 +1,5 @@
 import functools
+import math
 
 import jax
 import jax.numpy as jnp
@@ -21,7 +22,7 @@
 REACH = 2
 GROUP = 6
 SHARE = 4
-UNROLL = 8
+UNROLL = 16
 
 VMEM = pl.BlockSpec(memory_space=pltpu.VMEM)
 SMEM = pl.BlockSpec(memory_space=pltpu.SMEM)
@@ -60,35 +61,30 @@
     copy.wait()
 
 
-def load_kernel(state, block, face_a, rows, corner_a, corner_b, sems):
+def rims_kernel(state, face_a, rows, corner_a, corner_b):
     fields, width = state.shape[:2]
     even = is_even()
-    last = width - REACH
-    copies = [
-        pltpu.make_async_copy(state.at[g], block.at[g], sems.at[g]) for g in range(fields)
-    ]
-    for copy in copies:
-        copy.start()
+    face_a[...] = state[:, pl.ds(jnp.where(even, width - REACH, 0), REACH)]
     row = iota((TILE, LANES), 0)
     outer = (row < REACH) | (row >= TILE - REACH)
+    for g in range(fields):
+        for pair in range(width // 2):
+            first = edge_tile(state, g, 2 * pair)
+            second = edge_tile(state, g, 2 * pair + 1)
+            rows[g, pair] = jnp.where(outer, first, pltpu.roll(second, TILE // 2, 0))
     near_a = jnp.where(even, width - 1, 0)
     near_b = jnp.where(even, 0, width - 1)
-    held = [None, None]
-    for g in range(fields):
-        copies[g].wait()
-        face_a[g] = block[g, pl.ds(jnp.where(even, last, 0), REACH)]
-        for pair in range(width // 2):
-            first = edge_tile(block, g, 2 * pair)
-            second = edge_tile(block, g, 2 * pair + 1)
-            rows[g, pair] = jnp.where(outer, first, pltpu.roll(second, TILE // 2, 0))
-        t, k = g // SHARE, g % SHARE
-        for n, (corner, x) in enumerate(((corner_a, near_a), (corner_b, near_b))):
-            tile = edge_tile(block, g, x)
-            if k:
-                tile = jnp.where(corner_rows(k), pltpu.roll(tile, 2 * k, 0), held[n])
-            held[n] = tile
-            if k == SHARE - 1 or g == fields - 1:
-                corner[t] = tile
+    for corner, x in ((corner_a, near_a), (corner_b, near_b)):
+        for t in range(corner.shape[0]):
+            held = None
+            for k in range(SHARE):
+                g = t * SHARE + k
+                if g < fields:
+                    tile = edge_tile(state, g, x)
+                    if k:
+                        tile = jnp.where(corner_rows(k), pltpu.roll(tile, 2 * k, 0), held)
+                    held = tile
+            corner[t] = held
 
 
 def bottom_mask(active):
@@ -222,6 +218,7 @@
     grains = fields - 1
     rows = height + TILE
     top = height + TILE
+    unroll = math.gcd(width, UNROLL)
     span = float(length * lax.axis_size("gz"))
     base = lax.axis_index("gz") * length
     lane = iota((1, LANES), 1)
@@ -294,10 +291,10 @@
     def plane_of(x):
         return lambda g: jnp.concatenate([first[g, x, own], first[g, x, 0:TILE]], axis=0)
 
-    @pl.loop(0, width // UNROLL)
+    @pl.loop(0, width // unroll)
     def _(block):
-        for part in range(UNROLL):
-            x = block * UNROLL + part
+        for part in range(unroll):
+            x = block * unroll + part
             now, after = rims[part % 2], rims[1 - part % 2]
             put_lower((x + 1) * GROUP + REACH, plane_of(x))
             plane_first(x + REACH, lambda g: zsum[g, x], lambda g: now[g])
@@ -318,10 +315,10 @@
         for g in range(fields):
             done[g, x] = pltpu.roll(held[g], LANES - REACH, 1)
 
-    @pl.loop(0, width // UNROLL)
+    @pl.loop(0, width // unroll)
     def _(block):
-        for part in range(UNROLL):
-            x = block * UNROLL + part
+        for part in range(unroll):
+            x = block * unroll + part
             now, after = part % 2, 1 - part % 2
             flush(pending[after], jnp.maximum(x - 1, 0))
             full = [first[g, x + 1, own] for g in range(fields)]
@@ -445,31 +442,26 @@
             for d in toward
         ]
 
-    held = pltpu.with_memory_space_constraint(state, pltpu.HBM)
-    in_hbm = [pl.BlockSpec(memory_space=pltpu.HBM)]
     face = shape(fields, REACH, height, length)
     face_b = call(
         outer_face_kernel,
         face,
-        [held],
+        [pltpu.with_memory_space_constraint(state, pltpu.HBM)],
         100000,
-        specs=in_hbm,
+        specs=[pl.BlockSpec(memory_space=pltpu.HBM)],
         scratch=[pltpu.SemaphoreType.DMA(())],
     )
     got_b = swap(face_b, [(i, (i + 1) % count_x) for i in range(1, count_x, 2)])
-    block, face_a, edge, corner_a, corner_b = call(
-        load_kernel,
+    face_a, edge, corner_a, corner_b = call(
+        rims_kernel,
         [
-            whole,
             face,
             shape(fields, width // 2, TILE, length),
             shape(groups, TILE, length),
             shape(groups, TILE, length),
         ],
-        [held],
+        [state],
         100000,
-        specs=in_hbm,
-        scratch=[pltpu.SemaphoreType.DMA((fields,))],
     )
     near = [
         lax.ppermute(edge, "gy", [(j, (j + d) % count_y) for j in range(count_y)])
@@ -481,7 +473,7 @@
     zsum, own, marks = call(
         prepare_kernel,
         [whole, shape(fields, height, length), shape(rows, length)],
-        [block, seeds, frame_shifts],
+        [state, seeds, frame_shifts],
         5000000,
         specs=[VMEM, VMEM, SMEM],
     )
@@ -491,7 +483,7 @@
     done, lower = call(
         functools.partial(bulk_kernel, merged),
         [whole, packed],
-        [block, zsum, mobility, frame_shifts, *halo],
+        [state, zsum, mobility, frame_shifts, *halo],
         20000000,
         specs=[VMEM, VMEM, SMEM, SMEM] + [VMEM] * len(halo),
         scratch=[

time: 25.3 us -> 24.4 us (0.964)
  Pallas kernels: 9.25 us -> 7.54 us
  local copies, waits for them, and re-layouts: 0.11 us -> 1.38 us
  waiting for transfers between devices: 3.54 us -> 2.56 us
  starting transfers between devices: 12.2 us -> 12.6 us
    pallas_call x6, Pallas kernels: 9.25 us -> 7.54 us  [call(): pl.pallas_call(kernel, out_shape=outs, in_specs=specs or [VMEM] * len(inp...]
    ppermute x2, waiting for transfers between devices: 3.17 us -> 1.85 us  [diagonal(): lax.ppermute(value, ('gx', 'gy'), [(i * count_y + j, partner(i, kind) * c...]
    unnamed x7 -> x11, local copies, waits for them, and re-layouts: 0.11 us -> 1.38 us
    ppermute x1, starting transfers between devices: 4.25 us -> 4.68 us  [shards(): above = lax.ppermute(slab, 'gz', [(k, k - 1) for k in range(1, count_z)])]
    ppermute x1, waiting for transfers between devices: 0.36 us -> 0.71 us  [shards(): above = lax.ppermute(slab, 'gz', [(k, k - 1) for k in range(1, count_z)])]
where the time goes in v4:
time: 24.4 us; the launch traced here: 24.2 us
  starting transfers between devices  12.6 us (52%)
  Pallas kernels  7.54 us (31%)
  waiting for transfers between devices  2.56 us (10%)
  local copies, waits for them, and re-layouts  1.38 us (6%)
    pallas_call x6, Pallas kernels, call(): pl.pallas_call(kernel, out_shape=outs, in_specs=specs or [VMEM] * len(inp...  7.54 us
    ppermute x1, starting transfers between devices, shards(): above = lax.ppermute(slab, 'gz', [(k, k - 1) for k in range(1, count_z)])  4.68 us
    ppermute x2, starting transfers between devices, swap(): return lax.ppermute(value, 'gx', pairs + [(j, i) for i, j in pairs])  3.56 us
    ppermute x2, starting transfers between devices, diagonal(): lax.ppermute(value, ('gx', 'gy'), [(i * count_y + j, partner(i, kind) * c...  2.27 us
    ppermute x1, starting transfers between devices, shards(): lax.ppermute(edge, 'gy', [(j, (j + d) % count_y) for j in range(count_y)])  2.12 us
    ppermute x2, waiting for transfers between devices, diagonal(): lax.ppermute(value, ('gx', 'gy'), [(i * count_y + j, partner(i, kind) * c...  1.85 us
    unnamed x11, local copies, waits for them, and re-layouts  1.38 us
    ppermute x1, waiting for transfers between devices, shards(): above = lax.ppermute(slab, 'gz', [(k, k - 1) for k in range(1, count_z)])  0.71 us
  transfers between devices with their start and end apart: 6, of which 2 were waited for; matrix products, arithmetic and copies ran while one was open for 0% of the time, Pallas kernels for 22%

profile of v4, /device:TPU:1, one launch (start us, length us, event | category | flops | bytes accessed | tf_op | source)
XLA Modules:
  0.0 24.2 jit_solution(1957505167606794392)
XLA Ops:
  0.0 0.0 copy-start
  0.0 1.3 %copy-done = f32[9,16,16,128]{3,2,1,0:T(8,128)S(1)} copy-done((f32[9,16,16,128]{3,2,1,0:T(8,128)S(1)}, f32[9,16,16,128]{3,2,1,0:T(8,128)}, u32[]{:S(2)}) %copy-start) | copy-done | bytes 1179672
  1.3 0.0 copy-start.4
  1.3 0.0 copy-start.1
  1.3 0.0 copy-start.2
  1.3 0.1 shard_map.47
  1.4 2.1 %collective-permute-start.2 = (f32[9,8,8,128]{3,2,1,0:T(8,128)S(1)}, f32[9,8,8,128]{3,2,1,0:T(8,128)S(1)}, u32[]{:S(2)}, u32[]{:S(2)}) collective-permute-start(f32[9,8,8,128]{3,2,1,0:T(8,128)S(1)} %get-tuple-element.16), channel_id=1, source_target_pairs={{0,4},{4,0},{1,5},{5,1},{2,6},{6,2},{3,7},{7,3},{8,12},{12,8},{9,1... | collective-permute-start | bytes 884744 | tf_op jit(solution)/shard_map/ppermute | solution.py:467
  3.5 1.3 %collective-permute-start = (f32[9,2,16,128]{3,2,1,0:T(8,128)S(1)}, f32[9,2,16,128]{3,2,1,0:T(8,128)S(1)}, u32[]{:S(2)}, u32[]{:S(2)}) collective-permute-start(f32[9,2,16,128]{3,2,1,0:T(8,128)S(1)} %get-tuple-element.15), channel_id=1, source_target_pairs={{0,8},{16,24},{8,0},{24,16},{1,9},{17,25},{9,1},{25,17},{2,10},{18... | collective-permute-start | bytes 442376 | tf_op jit(solution)/shard_map/ppermute | solution.py:427
  4.8 0.9 %shard_map.48 = f32[9,2,16,128]{3,2,1,0:T(8,128)S(1)} custom-call(f32[9,16,16,128]{3,2,1,0:T(8,128)} %state.7), custom_call_target="tpu_custom_call" | custom-call | flops 100000 | bytes 100000 | tf_op jit(solution)/shard_map/pallas_call | solution.py:403
  5.7 0.0 copy-start.3
  5.7 2.3 %collective-permute-start.1 = (f32[9,2,16,128]{3,2,1,0:T(8,128)S(1)}, f32[9,2,16,128]{3,2,1,0:T(8,128)S(1)}, u32[]{:S(2)}, u32[]{:S(2)}) collective-permute-start(f32[9,2,16,128]{3,2,1,0:T(8,128)S(1)} %shard_map.48), channel_id=1, source_target_pairs={{8,16},{24,0},{16,8},{0,24},{9,17},{25,1},{17,9},{1,25},{10,18},{2... | collective-permute-start | bytes 442376 | tf_op jit(solution)/shard_map/ppermute | solution.py:427
  8.0 0.3 %collective-permute-start.3 = (f32[3,8,128]{2,1,0:T(8,128)S(1)}, f32[3,8,128]{2,1,0:T(8,128)S(1)}, u32[]{:S(2)}, u32[]{:S(2)}) collective-permute-start(f32[3,8,128]{2,1,0:T(8,128)S(1)} %get-tuple-element.17), channel_id=1, source_target_pairs={{0,12},{4,8},{8,4},{12,0},{16,28},{20,24},{24,20},{28,16},{1,13},{... | collective-permute-start | bytes 36872 | tf_op jit(solution)/shard_map/ppermute | solution.py:433
  8.3 1.9 %collective-permute-start.4 = (f32[3,8,128]{2,1,0:T(8,128)S(1)}, f32[3,8,128]{2,1,0:T(8,128)S(1)}, u32[]{:S(2)}, u32[]{:S(2)}) collective-permute-start(f32[3,8,128]{2,1,0:T(8,128)S(1)} %get-tuple-element.18), channel_id=1, source_target_pairs={{0,28},{4,24},{8,20},{12,16},{16,12},{20,8},{24,4},{28,0},{1,29},{... | collective-permute-start | bytes 36872 | tf_op jit(solution)/shard_map/ppermute | solution.py:433
  10.2 0.0 copy-done.4
  10.2 0.1 copy.5.seeds
  10.4 0.0 copy-done.1
  10.4 0.0 copy-done.2
  10.4 1.5 %shard_map.46 = (f32[9,16,16,128]{3,2,1,0:T(8,128)S(1)}, f32[9,16,128]{2,1,0:T(8,128)S(1)}, f32[24,128]{1,0:T(8,128)S(1)}) custom-call(f32[9,16,16,128]{3,2,1,0:T(8,128)S(1)} %copy-done.1, s32[2,2,64,32]{3,2,1,0:T(8,128)S(1)} %copy.5.seeds, s32[2]{0:T(128)S(1)} %copy-done.2), custom_call_target="tpu_custom_call" | custom-call | flops 5000000 | bytes 5000000 | tf_op jit(solution)/shard_map/pallas_call | solution.py:403
  11.9 0.0 collective-permute-done.3.rest_1_
  11.9 1.8 %collective-permute-done.4.rest_2_ = f32[3,8,128]{2,1,0:T(8,128)S(1)} collective-permute-done((f32[3,8,128]{2,1,0:T(8,128)S(1)}, f32[3,8,128]{2,1,0:T(8,128)S(1)}, u32[]{:S(2)}, u32[]{:S(2)}) %collective-permute-start.4) | collective-permute-done | bytes 12320 | tf_op jit(solution)/shard_map/ppermute | solution.py:433
  13.7 0.0 collective-permute-done.face_a
  13.7 0.0 collective-permute-done.1.face_b
  13.8 0.0 collective-permute-done.2.rest_0_
  13.8 0.3 %shard_map.50.slab = f32[9,24,128]{2,1,0:T(8,128)S(1)} custom-call(f32[9,16,128]{2,1,0:T(8,128)S(1)} %get-tuple-element.20.own, f32[9,2,16,128]{3,2,1,0:T(8,128)S(1)} %collective-permute-done.face_a, f32[9,2,16,128]{3,2,1,0:T(8,128)S(1)} %collective-permute-done.1.face_b, f32[9,8,8,128]{3,2,1,0:T(8,128)S(1)} %collective-permute-done.2.rest_0_, ...), custom_call_target="tpu_custom_call" | custom-call | flops 100000 | bytes 100000 | tf_op jit(solution)/shard_map/pallas_call | solution.py:403
  14.1 4.7 %collective-permute-start.5 = (f32[9,24,128]{2,1,0:T(8,128)S(1)}, f32[9,24,128]{2,1,0:T(8,128)S(1)}, u32[]{:S(2)}, u32[]{:S(2)}) collective-permute-start(f32[9,24,128]{2,1,0:T(8,128)S(1)} %shard_map.50.slab), channel_id=1, source_target_pairs={{1,0},{2,1},{3,2},{5,4},{6,5},{7,6},{9,8},{10,9},{11,10},{13,12},{... | collective-permute-start | bytes 331784 | tf_op jit(solution)/shard_map/ppermute | solution.py:482
  18.8 0.0 copy-done.3
  18.8 2.8 %shard_map.49 = (f32[9,16,16,128]{3,2,1,0:T(8,128)S(1)}, f32[9,24,128]{2,1,0:T(8,128)S(1)}) custom-call(f32[9,16,16,128]{3,2,1,0:T(8,128)S(1)} %copy-done.1, f32[9,16,16,128]{3,2,1,0:T(8,128)S(1)} %get-tuple-element.14.zsum, f32[8]{0:T(128)S(1)} %copy-done.3, s32[2]{0:T(128)S(1)} %copy-done.2, f32[9,2,16,128]{3,2,1,0:T(8,128)S(1)} %collective-permute-done.face_a, ...), custom_call_target="tpu_custom_call" | custom-call | flops 20000000 | bytes 20000000 | tf_op jit(solution)/shard_map/pallas_call | solution.py:403
  21.6 0.7 %collective-permute-done.5.above = f32[9,24,128]{2,1,0:T(8,128)S(1)} collective-permute-done((f32[9,24,128]{2,1,0:T(8,128)S(1)}, f32[9,24,128]{2,1,0:T(8,128)S(1)}, u32[]{:S(2)}, u32[]{:S(2)}) %collective-permute-start.5) | collective-permute-done | bytes 110624 | tf_op jit(solution)/shard_map/ppermute | solution.py:482
  22.3 1.9 %shard_map.51 = f32[9,16,16,128]{3,2,1,0:T(8,128)} custom-call(f32[9,16,16,128]{3,2,1,0:T(8,128)S(1)} %get-tuple-element.19.done, f32[9,24,128]{2,1,0:T(8,128)S(1)} %shard_map.50.slab, f32[9,24,128]{2,1,0:T(8,128)S(1)} %collective-permute-done.5.above, f32[9,24,128]{2,1,0:T(8,128)S(1)} %get-tuple-element.21.lower, f32[24,128]{1,0:T(8,128)S(1)} %get-tuple-element.22.marks, ...), custom_call_target="tpu_custom_call" | custom-call | flops 100000 | bytes 100000 | tf_op jit(solution)/shard_map/pallas_call | solution.py:403
Async XLA Ops:
  0.0 1.3 %copy-start = (f32[9,16,16,128]{3,2,1,0:T(8,128)S(1)}, f32[9,16,16,128]{3,2,1,0:T(8,128)}, u32[]{:S(2)}) copy-start(f32[9,16,16,128]{3,2,1,0:T(8,128)} %state.7) | copy-start | bytes 3538948
  1.3 9.0 %copy-start.4 = (s32[2,2,64,32]{2,3,1,0:T(8,128)S(1)}, s32[2,2,64,32]{2,3,1,0:T(8,128)}, u32[]{:S(2)}) copy-start(s32[2,2,64,32]{2,3,1,0:T(8,128)} %param.6) | copy-start | bytes 98308
  1.3 9.1 %copy-start.1 = (f32[9,16,16,128]{3,2,1,0:T(8,128)S(1)}, f32[9,16,16,128]{3,2,1,0:T(8,128)}, u32[]{:S(2)}) copy-start(f32[9,16,16,128]{3,2,1,0:T(8,128)} %state.7) | copy-start | bytes 3538948
  1.3 9.1 %copy-start.2 = (s32[2]{0:T(128)S(1)}, s32[2]{0:T(128)}, u32[]{:S(2)}) copy-start(s32[2]{0:T(128)} %shifts.5) | copy-start | bytes 28
  1.4 12.4 %collective-permute-start.2 = (f32[9,8,8,128]{3,2,1,0:T(8,128)S(1)}, f32[9,8,8,128]{3,2,1,0:T(8,128)S(1)}, u32[]{:S(2)}, u32[]{:S(2)}) collective-permute-start(f32[9,8,8,128]{3,2,1,0:T(8,128)S(1)} %get-tuple-element.16), channel_id=1, source_target_pairs={{0,4},{4,0},{1,5},{5,1},{2,6},{6,2},{3,7},{7,3},{8,12},{12,8},{9,1... | collective-permute-start | bytes 884744 | tf_op jit(solution)/shard_map/ppermute | solution.py:467
  3.5 10.3 %collective-permute-start = (f32[9,2,16,128]{3,2,1,0:T(8,128)S(1)}, f32[9,2,16,128]{3,2,1,0:T(8,128)S(1)}, u32[]{:S(2)}, u32[]{:S(2)}) collective-permute-start(f32[9,2,16,128]{3,2,1,0:T(8,128)S(1)} %get-tuple-element.15), channel_id=1, source_target_pairs={{0,8},{16,24},{8,0},{24,16},{1,9},{17,25},{9,1},{25,17},{2,10},{18... | collective-permute-start | bytes 442376 | tf_op jit(solution)/shard_map/ppermute | solution.py:427
  5.7 13.1 %copy-start.3 = (f32[8]{0:T(128)S(1)}, f32[8]{0:T(128)}, u32[]{:S(2)}) copy-start(f32[8]{0:T(128)} %mobility.3) | copy-start | bytes 100
  5.7 8.0 %collective-permute-start.1 = (f32[9,2,16,128]{3,2,1,0:T(8,128)S(1)}, f32[9,2,16,128]{3,2,1,0:T(8,128)S(1)}, u32[]{:S(2)}, u32[]{:S(2)}) collective-permute-start(f32[9,2,16,128]{3,2,1,0:T(8,128)S(1)} %shard_map.48), channel_id=1, source_target_pairs={{8,16},{24,0},{16,8},{0,24},{9,17},{25,1},{17,9},{1,25},{10,18},{2... | collective-permute-start | bytes 442376 | tf_op jit(solution)/shard_map/ppermute | solution.py:427
  8.0 3.9 %collective-permute-start.3 = (f32[3,8,128]{2,1,0:T(8,128)S(1)}, f32[3,8,128]{2,1,0:T(8,128)S(1)}, u32[]{:S(2)}, u32[]{:S(2)}) collective-permute-start(f32[3,8,128]{2,1,0:T(8,128)S(1)} %get-tuple-element.17), channel_id=1, source_target_pairs={{0,12},{4,8},{8,4},{12,0},{16,28},{20,24},{24,20},{28,16},{1,13},{... | collective-permute-start | bytes 36872 | tf_op jit(solution)/shard_map/ppermute | solution.py:433
  8.3 5.4 %collective-permute-start.4 = (f32[3,8,128]{2,1,0:T(8,128)S(1)}, f32[3,8,128]{2,1,0:T(8,128)S(1)}, u32[]{:S(2)}, u32[]{:S(2)}) collective-permute-start(f32[3,8,128]{2,1,0:T(8,128)S(1)} %get-tuple-element.18), channel_id=1, source_target_pairs={{0,28},{4,24},{8,20},{12,16},{16,12},{20,8},{24,4},{28,0},{1,29},{... | collective-permute-start | bytes 36872 | tf_op jit(solution)/shard_map/ppermute | solution.py:433
  14.1 8.2 %collective-permute-start.5 = (f32[9,24,128]{2,1,0:T(8,128)S(1)}, f32[9,24,128]{2,1,0:T(8,128)S(1)}, u32[]{:S(2)}, u32[]{:S(2)}) collective-permute-start(f32[9,24,128]{2,1,0:T(8,128)S(1)} %shard_map.50.slab), channel_id=1, source_target_pairs={{1,0},{2,1},{3,2},{5,4},{6,5},{7,6},{9,8},{10,9},{11,10},{13,12},{... | collective-permute-start | bytes 331784 | tf_op jit(solution)/shard_map/ppermute | solution.py:482

commit v5 on v4

--- a/solution.py
+++ b/solution.py
@@ -95,6 +95,17 @@
     return pltpu.roll(p, 1, 1) * mask + pltpu.roll(p, LANES - 1, 1)
 
 
+def heights(length, shift):
+    span = float(length * lax.axis_size("gz"))
+    zpos = lax.axis_index("gz") * length + iota((1, LANES), 1) - shift
+    return 1.0 - 2.0 * (zpos.astype(jnp.float32) + 0.5) / span
+
+
+def step_of(center, sums, theta, speeds):
+    grains = len(center) - 1
+    return relax(center[:grains], center[grains], sums[:grains], sums[grains], theta, speeds)
+
+
 def early_mask(shifts):
     return bottom_mask((lax.axis_index("gz") == 0) & (shifts[0] > 0))
 
@@ -103,20 +114,44 @@
     return (slot * GROUP + REACH) % LANES
 
 
-def prepare_kernel(state, seeds, shifts, zsum, own, marks):
-    fields, width, height, _ = state.shape
+def prepare_kernel(state, seeds, mobility, shifts, part, outer, own, below, marks, *sums):
+    fields, width, height, length = state.shape
     rows = height + TILE
     total_x, total_y = seeds.shape[2:]
     slot, place = group_and_slot()
+    ahead, _ = group_and_slot(1)
     mask = early_mask(shifts)
-    for g in range(fields):
-        held = None
-        for x in range(width):
-            p = state[g, x]
-            zsum[g, x] = along(p, mask)
-            moved = pltpu.roll(p, slot_shift(x + REACH), 1)
-            held = moved if held is None else jnp.where(slot == x + REACH, moved, held)
-        own[g] = held
+    theta = heights(length, shifts[0])
+    speeds = [mobility[g] for g in range(fields - 1)]
+    flat = state.reshape(fields * width * height, LANES)
+
+    def lateral(g, x):
+        start = (g * width + x) * height
+        total = state[g, x - 1] + state[g, x + 1]
+        return total + flat[start - 1 : start - 1 + height] + flat[start + 1 : start + 1 + height]
+
+    for g in range(fields):
+        sums[1][g] = along(state[g, 1], mask)
+        outer[g, 0] = along(state[g, 0], mask)
+        outer[g, 1] = along(state[g, width - 1], mask)
+        below[g] = jnp.zeros((height, LANES), jnp.float32)
+        own[g] = jnp.zeros((height, LANES), jnp.float32)
+    for x in range(width):
+        now, after = sums[x % 2], sums[1 - x % 2]
+        for g in range(fields):
+            moved = pltpu.roll(state[g, x], slot_shift(x + REACH), 1)
+            own[g] = jnp.where(slot == x + REACH, moved, own[g])
+            if 1 < x:
+                moved = pltpu.roll(part[g, x - 2], slot_shift(x - 1 + REACH), 1)
+                below[g] = jnp.where(ahead == x - 1 + REACH, moved, below[g])
+        if 0 < x < width - 1:
+            center = [state[g, x] for g in range(fields)]
+            around = [lambda g=g: lateral(g, x) + now[g] for g in range(fields)]
+            fresh = step_of(center, around, theta, speeds)
+            for g in range(fields):
+                part[g, x - 1] = fresh[g]
+                if x + 1 < width - 1:
+                    after[g] = along(state[g, x + 1], mask)
 
     step = jnp.where(shifts[0] > 0, 0, 1)
     row_y = iota((rows, total_y), 0)
@@ -210,101 +245,109 @@
     return fresh
 
 
-def bulk_kernel(merged, state, zsum, mobility, shifts, face_a, face_b, *rest):
-    done, lower, wide, first = rest[-10:-6]
-    rims, sums, pending = rest[-6:-4], rest[-4:-2], rest[-2:]
-    halo = Halo(merged, face_a, face_b, rest[:-10])
+def bulk_kernel(merged, state, part, outer, below, mobility, shifts, face_a, face_b, *rest):
+    done, lower, first, edge, edge_sum, edge_new, beyond = rest[-11:-4]
+    sums, pending = rest[-4:-2], rest[-2:]
+    halo = Halo(merged, face_a, face_b, rest[:-11])
     fields, width, height, length = state.shape
-    grains = fields - 1
-    rows = height + TILE
     top = height + TILE
     unroll = math.gcd(width, UNROLL)
-    span = float(length * lax.axis_size("gz"))
-    base = lax.axis_index("gz") * length
-    lane = iota((1, LANES), 1)
-    slot_of, _ = group_and_slot(1)
-    speeds = [mobility[g] for g in range(grains)]
+    chunk = next(c for c in (3, 2, 1) if (width + 2) % c == 0)
+    ahead, _ = group_and_slot(1)
+    speeds = [mobility[g] for g in range(fields - 1)]
     own = slice(TILE, TILE + height)
-
-    def theta_of(shift):
-        zpos = (base + lane - shift).astype(jnp.float32)
-        return 1.0 - 2.0 * (zpos + 0.5) / span
-
-    def put_rim(ref, g, x, tile):
-        ref[g, x, 0:TILE] = tile
-        ref[g, x, top : top + TILE] = tile
-
-    for g in range(fields):
-        for x in range(width):
-            wide[g, x + REACH, own] = state[g, x]
-        for side in range(2):
-            for n in range(REACH):
-                wide[g, n + side * (width + REACH), own] = halo.face(g, side, n)
+    row = iota((TILE, LANES), 0)
+    half = row < TILE // 2
+    mask_first = early_mask(shifts)
+    theta_first = heights(length, shifts[0])
+
+    def plane(g, x):
+        if 0 <= x < width:
+            return state[g, x]
+        return halo.face(g, 0, x + REACH) if x < 0 else halo.face(g, 1, x - width)
+
+    def fold(p, rim):
+        low, high = p[0:TILE], p[height - TILE : height]
+        upper = pltpu.roll(jnp.where(half, rim, high), REACH, 0)
+        under = pltpu.roll(jnp.where(half, low, rim), TILE - REACH, 0)
+        return jnp.where(half, upper, under)
+
+    for g in range(fields):
         for n in range(width // 2):
-            first_tile, second_tile = halo.pair(g, n)
-            put_rim(wide, g, 2 * n + REACH, first_tile)
-            put_rim(wide, g, 2 * n + 1 + REACH, second_tile)
-        put_rim(wide, g, REACH - 1, halo.corner(g, 0))
-        put_rim(wide, g, width + REACH, halo.corner(g, 1))
-        for x in (0, width + 2 * REACH - 1):
-            put_rim(wide, g, x, jnp.zeros((TILE, LANES), jnp.float32))
-
-    mask_first = early_mask(shifts)
-    theta_first = theta_of(shifts[0])
-
-    def lateral(ref, g, x, with_rim):
-        total = ref[g, x - 1, own] + ref[g, x + 1, own]
-        total = total + ref[g, x, TILE - 1 : top - 1] + ref[g, x, TILE + 1 : top + 1]
-        if not with_rim:
-            return total
-        rim = ref[g, x - 1, 0:TILE] + ref[g, x + 1, 0:TILE]
-        rim = rim + ref[g, x, top - 1 : top - 1 + TILE] + ref[g, x, 1 : TILE + 1]
-        return jnp.concatenate([total, rim], axis=0)
-
-    def plane_first(x, zsum_own, zsum_rim):
-        full = [wide[g, x, TILE : top + TILE] for g in range(fields)]
-        parts = [
-            lambda g=g: lateral(wide, g, x, True)
-            + jnp.concatenate([zsum_own(g), zsum_rim(g)], axis=0)
-            for g in range(fields)
-        ]
-        fresh = relax(full[:grains], full[grains], parts[:grains], parts[grains], theta_first, speeds)
+            for x, rim in zip((2 * n, 2 * n + 1), halo.pair(g, n)):
+                edge[g, x + REACH] = fold(state[g, x], rim)
+        for side, x in ((0, -1), (1, width)):
+            edge[g, x + REACH] = fold(plane(g, x), halo.corner(g, side))
+            beyond[g, side] = along(plane(g, x), mask_first)
+        for x in (-REACH, width + REACH - 1):
+            p = plane(g, x)
+            edge[g, x + REACH] = fold(p, p[0:TILE])
+        for x in range(1, width - 1):
+            first[g, x + 1, own] = part[g, x - 1]
+    for g in range(fields):
+        for i in range(width + 2):
+            edge_sum[g, i] = along(edge[g, i + 1], mask_first)
+
+    for x in (-1, 0, width - 1, width):
+        zsums, side = (outer, int(x > 0)) if 0 <= x < width else (beyond, int(x > 0))
+
+        def around(g):
+            center = plane(g, x)
+            total = plane(g, x - 1) + plane(g, x + 1) + zsums[g, side]
+            return total + pltpu.roll(center, 1, 0) + pltpu.roll(center, height - 1, 0)
+
+        center = [plane(g, x) for g in range(fields)]
+        parts = [functools.partial(around, g) for g in range(fields)]
+        fresh = step_of(center, parts, theta_first, speeds)
         for g in range(fields):
-            first[g, x - 1, own] = fresh[g][0:height]
-            put_rim(first, g, x - 1, fresh[g][height:rows])
-
-    def put_lower(slot, source):
+            first[g, x + 1, own] = fresh[g]
+
+    for i in range(0, width + 2, chunk):
+
+        def tiles(ref, g, start):
+            return jnp.concatenate([ref[g, start + t] for t in range(chunk)], axis=0)
+
+        def turned(g, shift):
+            return jnp.concatenate(
+                [pltpu.roll(edge[g, i + 1 + t], shift, 0) for t in range(chunk)], axis=0
+            )
+
+        def around(g):
+            total = tiles(edge, g, i) + tiles(edge, g, i + 2) + tiles(edge_sum, g, i)
+            return total + turned(g, 1) + turned(g, TILE - 1)
+
+        center = [tiles(edge, g, i + 1) for g in range(fields)]
+        parts = [functools.partial(around, g) for g in range(fields)]
+        fresh = step_of(center, parts, theta_first, speeds)
         for g in range(fields):
-            moved = pltpu.roll(source(g), slot, 1)
-            lower[g] = jnp.where(slot_of * GROUP + REACH == slot, moved, lower[g])
-
-    lower[...] = jnp.zeros_like(lower)
-    for x in (1, width + REACH):
-        plane_first(
-            x,
-            lambda g, x=x: along(wide[g, x, own], mask_first),
-            lambda g, x=x: along(wide[g, x, 0:TILE], mask_first),
+            for t in range(chunk):
+                tile = fresh[g][t * TILE : (t + 1) * TILE]
+                edge_new[g, i + t] = tile
+                first[g, i + t, top - 1 : top + 1] = tile[1:3]
+                first[g, i + t, TILE - 1 : TILE + 1] = tile[5:7]
+
+    for g in range(fields):
+        held = below[g]
+        for x in (-1, 0, width - 1, width):
+            moved = pltpu.roll(first[g, x + 1, own], slot_shift(x + REACH), 1)
+            held = jnp.where(ahead == x + REACH, moved, held)
+        rim = jnp.zeros((TILE, LANES), jnp.float32)
+        for i in range(width + 2):
+            moved = pltpu.roll(edge_new[g, i], slot_shift(i + 1), 1)
+            rim = jnp.where(ahead == i + 1, moved, rim)
+        forward, back = pltpu.roll(rim, REACH, 0), pltpu.roll(rim, TILE - REACH, 0)
+        lower[g, 0:height] = held
+        lower[g, 0:TILE] = jnp.where(row == 0, forward, held[0:TILE])
+        lower[g, height - TILE : height] = jnp.where(
+            row == TILE - 1, back, held[height - TILE : height]
         )
-    for g in range(fields):
-        rims[0][g] = along(wide[g, REACH, 0:TILE], mask_first)
-
-    def plane_of(x):
-        return lambda g: jnp.concatenate([first[g, x, own], first[g, x, 0:TILE]], axis=0)
-
-    @pl.loop(0, width // unroll)
-    def _(block):
-        for part in range(unroll):
-            x = block * unroll + part
-            now, after = rims[part % 2], rims[1 - part % 2]
-            put_lower((x + 1) * GROUP + REACH, plane_of(x))
-            plane_first(x + REACH, lambda g: zsum[g, x], lambda g: now[g])
-            for g in range(fields):
-                after[g] = along(wide[g, x + REACH + 1, 0:TILE], mask_first)
-
-    for x in (width, width + 1):
-        put_lower((x + 1) * GROUP + REACH, plane_of(x))
-
-    theta_second = theta_of(REACH)
+        lower[g, height : height + TILE] = jnp.where(half, back, forward)
+
+    def lateral(g, x):
+        total = first[g, x - 1, own] + first[g, x + 1, own]
+        return total + first[g, x, TILE - 1 : top - 1] + first[g, x, TILE + 1 : top + 1]
+
+    theta_second = heights(length, REACH)
     mask_second = bottom_mask(lax.axis_index("gz") == 0)
 
     for g in range(fields):
@@ -322,12 +365,8 @@
             now, after = part % 2, 1 - part % 2
             flush(pending[after], jnp.maximum(x - 1, 0))
             full = [first[g, x + 1, own] for g in range(fields)]
-            parts = [
-                lambda g=g: lateral(first, g, x + 1, False) + sums[now][g] for g in range(fields)
-            ]
-            fresh = relax(
-                full[:grains], full[grains], parts[:grains], parts[grains], theta_second, speeds
-            )
+            parts = [lambda g=g: lateral(g, x + 1) + sums[now][g] for g in range(fields)]
+            fresh = step_of(full, parts, theta_second, speeds)
             for g in range(fields):
                 pending[now][g] = fresh[g]
                 sums[after][g] = along(first[g, x + 2, own], mask_second)
@@ -470,12 +509,16 @@
     got_a = swap(face_a, [(i, i + 1) for i in range(0, count_x, 2)])
     far_b = diagonal(corner_b, 1)
     far_a = diagonal(corner_a, 0)
-    zsum, own, marks = call(
+    sides = shape(fields, 2, height, length)
+    flat = shape(fields, height, length)
+    lines = pltpu.VMEM((fields, height, length), jnp.float32)
+    part, outer, own, below, marks = call(
         prepare_kernel,
-        [whole, shape(fields, height, length), shape(rows, length)],
-        [state, seeds, frame_shifts],
+        [shape(fields, width - 2, height, length), sides, flat, flat, shape(rows, length)],
+        [state, seeds, mobility, frame_shifts],
         5000000,
-        specs=[VMEM, VMEM, SMEM],
+        specs=[VMEM, VMEM, SMEM, SMEM],
+        scratch=[lines, lines],
     )
     halo = [got_a, got_b, *near, *far_a, *far_b]
     slab = call(functools.partial(slab_kernel, merged), packed, [own, *halo], 100000)
@@ -483,15 +526,20 @@
     done, lower = call(
         functools.partial(bulk_kernel, merged),
         [whole, packed],
-        [state, zsum, mobility, frame_shifts, *halo],
+        [state, part, outer, below, mobility, frame_shifts, *halo],
         20000000,
-        specs=[VMEM, VMEM, SMEM, SMEM] + [VMEM] * len(halo),
+        specs=[VMEM] * 4 + [SMEM, SMEM] + [VMEM] * len(halo),
         scratch=[
-            pltpu.VMEM((fields, width + 2 * REACH, rows + TILE, length), jnp.float32),
             pltpu.VMEM((fields, width + 2, rows + TILE, length), jnp.float32),
-        ]
-        + [pltpu.VMEM((fields, TILE, length), jnp.float32)] * 2
-        + [pltpu.VMEM((fields, height, length), jnp.float32)] * 4,
+            pltpu.VMEM((fields, width + 2 * REACH, TILE, length), jnp.float32),
+            pltpu.VMEM((fields, width + 2, TILE, length), jnp.float32),
+            pltpu.VMEM((fields, width + 2, TILE, length), jnp.float32),
+            pltpu.VMEM((fields, 2, height, length), jnp.float32),
+            lines,
+            lines,
+            lines,
+            lines,
+        ],
     )
     return call(
         crown_kernel,

time: 24.4 us -> 25.3 us (1.037)
  waiting for transfers between devices: 2.56 us -> 3.97 us
  starting transfers between devices: 12.6 us -> 12.1 us
    ppermute x2, waiting for transfers between devices: 1.85 us -> 2.92 us  [diagonal(): lax.ppermute(value, ('gx', 'gy'), [(i * count_y + j, partner(i, kind) * c...]
    ppermute x1, starting transfers between devices: 4.68 us -> 4.18 us  [shards(): above = lax.ppermute(slab, 'gz', [(k, k - 1) for k in range(1, count_z)])]
    ppermute x1, waiting for transfers between devices: 0.71 us -> 1.04 us  [shards(): above = lax.ppermute(slab, 'gz', [(k, k - 1) for k in range(1, count_z)])]
  transfers between devices with their start and end apart: 6 -> 6, of which waited for: 2 -> 2; matrix products, arithmetic and copies ran while one was open for 0% -> 0% of each run, Pallas kernels for 22% -> 21%
where the time goes in v5:
time: 25.3 us; the launch traced here: 25.1 us
  starting transfers between devices  12.1 us (48%)
  Pallas kernels  7.51 us (30%)
  waiting for transfers between devices  3.97 us (16%)
  local copies, waits for them, and re-layouts  1.38 us (5%)
    pallas_call x6, Pallas kernels, call(): pl.pallas_call(kernel, out_shape=outs, in_specs=specs or [VMEM] * len(inp...  7.51 us
    ppermute x1, starting transfers between devices, shards(): above = lax.ppermute(slab, 'gz', [(k, k - 1) for k in range(1, count_z)])  4.18 us
    ppermute x2, starting transfers between devices, swap(): return lax.ppermute(value, 'gx', pairs + [(j, i) for i, j in pairs])  3.39 us
    ppermute x2, waiting for transfers between devices, diagonal(): lax.ppermute(value, ('gx', 'gy'), [(i * count_y + j, partner(i, kind) * c...  2.92 us
    ppermute x2, starting transfers between devices, diagonal(): lax.ppermute(value, ('gx', 'gy'), [(i * count_y + j, partner(i, kind) * c...  2.44 us
    ppermute x1, starting transfers between devices, shards(): lax.ppermute(edge, 'gy', [(j, (j + d) % count_y) for j in range(count_y)])  2.12 us
    unnamed x11, local copies, waits for them, and re-layouts  1.38 us
    ppermute x1, waiting for transfers between devices, shards(): above = lax.ppermute(slab, 'gz', [(k, k - 1) for k in range(1, count_z)])  1.04 us
  transfers between devices with their start and end apart: 6, of which 2 were waited for; matrix products, arithmetic and copies ran while one was open for 0% of the time, Pallas kernels for 21%

profile of v5, /device:TPU:1, one launch (start us, length us, event | category | flops | bytes accessed | tf_op | source)
XLA Modules:
  0.0 25.1 jit_solution(7993456911895403518)
XLA Ops:
  0.0 0.0 copy-start
  0.0 1.3 %copy-done = f32[9,16,16,128]{3,2,1,0:T(8,128)S(1)} copy-done((f32[9,16,16,128]{3,2,1,0:T(8,128)S(1)}, f32[9,16,16,128]{3,2,1,0:T(8,128)}, u32[]{:S(2)}) %copy-start) | copy-done | bytes 1179672
  1.3 0.0 copy-start.4
  1.3 0.0 copy-start.1
  1.3 0.0 copy-start.2
  1.3 0.0 copy-start.3
  1.3 0.1 shard_map.47
  1.4 2.1 %collective-permute-start.2 = (f32[9,8,8,128]{3,2,1,0:T(8,128)S(1)}, f32[9,8,8,128]{3,2,1,0:T(8,128)S(1)}, u32[]{:S(2)}, u32[]{:S(2)}) collective-permute-start(f32[9,8,8,128]{3,2,1,0:T(8,128)S(1)} %get-tuple-element.20), channel_id=1, source_target_pairs={{0,4},{4,0},{1,5},{5,1},{2,6},{6,2},{3,7},{7,3},{8,12},{12,8},{9,1... | collective-permute-start | bytes 884744 | tf_op jit(solution)/shard_map/ppermute | solution.py:506
  3.5 0.9 %shard_map.48 = f32[9,2,16,128]{3,2,1,0:T(8,128)S(1)} custom-call(f32[9,16,16,128]{3,2,1,0:T(8,128)} %state.7), custom_call_target="tpu_custom_call" | custom-call | flops 100000 | bytes 100000 | tf_op jit(solution)/shard_map/pallas_call | solution.py:442
  4.4 3.4 %collective-permute-start.1 = (f32[9,2,16,128]{3,2,1,0:T(8,128)S(1)}, f32[9,2,16,128]{3,2,1,0:T(8,128)S(1)}, u32[]{:S(2)}, u32[]{:S(2)}) collective-permute-start(f32[9,2,16,128]{3,2,1,0:T(8,128)S(1)} %shard_map.48), channel_id=1, source_target_pairs={{8,16},{24,0},{16,8},{0,24},{9,17},{25,1},{17,9},{1,25},{10,18},{2... | collective-permute-start | bytes 442376 | tf_op jit(solution)/shard_map/ppermute | solution.py:466
  7.8 0.0 collective-permute-start
  7.8 1.4 %collective-permute-start.3 = (f32[3,8,128]{2,1,0:T(8,128)S(1)}, f32[3,8,128]{2,1,0:T(8,128)S(1)}, u32[]{:S(2)}, u32[]{:S(2)}) collective-permute-start(f32[3,8,128]{2,1,0:T(8,128)S(1)} %get-tuple-element.21), channel_id=1, source_target_pairs={{0,12},{4,8},{8,4},{12,0},{16,28},{20,24},{24,20},{28,16},{1,13},{... | collective-permute-start | bytes 36872 | tf_op jit(solution)/shard_map/ppermute | solution.py:472
  9.2 1.0 %collective-permute-start.4 = (f32[3,8,128]{2,1,0:T(8,128)S(1)}, f32[3,8,128]{2,1,0:T(8,128)S(1)}, u32[]{:S(2)}, u32[]{:S(2)}) collective-permute-start(f32[3,8,128]{2,1,0:T(8,128)S(1)} %get-tuple-element.22), channel_id=1, source_target_pairs={{0,28},{4,24},{8,20},{12,16},{16,12},{20,8},{24,4},{28,0},{1,29},{... | collective-permute-start | bytes 36872 | tf_op jit(solution)/shard_map/ppermute | solution.py:472
  10.2 0.0 copy-done.4
  10.2 0.1 copy.5.seeds
  10.3 0.0 copy-done.1
  10.4 0.0 copy-done.2
  10.4 0.0 copy-done.3
  10.4 1.8 %shard_map.46 = (f32[9,14,16,128]{3,2,1,0:T(8,128)S(1)}, f32[9,2,16,128]{3,2,1,0:T(8,128)S(1)}, f32[9,16,128]{2,1,0:T(8,128)S(1)}, f32[9,16,128]{2,1,0:T(8,128)S(1)}, f32[24,128]{1,0:T(8,128)S(1)}) custom-call(f32[9,16,16,128]{3,2,1,0:T(8,128)S(1)} %copy-done.1, s32[2,2,64,32]{3,2,1,0:T(8,128)S(1)} %copy.5.seeds, f32[8]{0:T(128)S(1)} %copy-done.2, ...), custom_call_target="tpu_custom_call" | custom-call | flops 5000000 | bytes 5000000 | tf_op jit(solution)/shard_map/pallas_call | solution.py:442
  12.2 2.9 %collective-permute-done.3.rest_1_ = f32[3,8,128]{2,1,0:T(8,128)S(1)} collective-permute-done((f32[3,8,128]{2,1,0:T(8,128)S(1)}, f32[3,8,128]{2,1,0:T(8,128)S(1)}, u32[]{:S(2)}, u32[]{:S(2)}) %collective-permute-start.3) | collective-permute-done | bytes 12320 | tf_op jit(solution)/shard_map/ppermute | solution.py:472
  15.1 0.0 collective-permute-done.4.rest_2_
  15.1 0.0 collective-permute-done.1.face_b
  15.1 0.0 collective-permute-done.face_a
  15.1 0.0 collective-permute-done.2.rest_0_
  15.1 0.3 %shard_map.50.slab = f32[9,24,128]{2,1,0:T(8,128)S(1)} custom-call(f32[9,16,128]{2,1,0:T(8,128)S(1)} %get-tuple-element.24.own, f32[9,2,16,128]{3,2,1,0:T(8,128)S(1)} %collective-permute-done.face_a, f32[9,2,16,128]{3,2,1,0:T(8,128)S(1)} %collective-permute-done.1.face_b, f32[9,8,8,128]{3,2,1,0:T(8,128)S(1)} %collective-permute-done.2.rest_0_, ...), custom_call_target="tpu_custom_call" | custom-call | flops 100000 | bytes 100000 | tf_op jit(solution)/shard_map/pallas_call | solution.py:442
  15.5 4.2 %collective-permute-start.5 = (f32[9,24,128]{2,1,0:T(8,128)S(1)}, f32[9,24,128]{2,1,0:T(8,128)S(1)}, u32[]{:S(2)}, u32[]{:S(2)}) collective-permute-start(f32[9,24,128]{2,1,0:T(8,128)S(1)} %shard_map.50.slab), channel_id=1, source_target_pairs={{1,0},{2,1},{3,2},{5,4},{6,5},{7,6},{9,8},{10,9},{11,10},{13,12},{... | collective-permute-start | bytes 331784 | tf_op jit(solution)/shard_map/ppermute | solution.py:525
  19.6 2.5 %shard_map.49 = (f32[9,16,16,128]{3,2,1,0:T(8,128)S(1)}, f32[9,24,128]{2,1,0:T(8,128)S(1)}) custom-call(f32[9,16,16,128]{3,2,1,0:T(8,128)S(1)} %copy-done.1, f32[9,14,16,128]{3,2,1,0:T(8,128)S(1)} %get-tuple-element.16.part, f32[9,2,16,128]{3,2,1,0:T(8,128)S(1)} %get-tuple-element.17.outer, f32[9,16,128]{2,1,0:T(8,128)S(1)} %get-tuple-element.18.below, ...), custom_call_target="tpu_custom_call" | custom-call | flops 20000000 | bytes 20000000 | tf_op jit(solution)/shard_map/pallas_call | solution.py:442
  22.1 1.0 %collective-permute-done.5.above = f32[9,24,128]{2,1,0:T(8,128)S(1)} collective-permute-done((f32[9,24,128]{2,1,0:T(8,128)S(1)}, f32[9,24,128]{2,1,0:T(8,128)S(1)}, u32[]{:S(2)}, u32[]{:S(2)}) %collective-permute-start.5) | collective-permute-done | bytes 110624 | tf_op jit(solution)/shard_map/ppermute | solution.py:525
  23.2 1.9 %shard_map.51 = f32[9,16,16,128]{3,2,1,0:T(8,128)} custom-call(f32[9,16,16,128]{3,2,1,0:T(8,128)S(1)} %get-tuple-element.23.done, f32[9,24,128]{2,1,0:T(8,128)S(1)} %shard_map.50.slab, f32[9,24,128]{2,1,0:T(8,128)S(1)} %collective-permute-done.5.above, f32[9,24,128]{2,1,0:T(8,128)S(1)} %get-tuple-element.25.lower, f32[24,128]{1,0:T(8,128)S(1)} %get-tuple-element.26.marks, ...), custom_call_target="tpu_custom_call" | custom-call | flops 100000 | bytes 100000 | tf_op jit(solution)/shard_map/pallas_call | solution.py:442
Async XLA Ops:
  0.0 1.3 %copy-start = (f32[9,16,16,128]{3,2,1,0:T(8,128)S(1)}, f32[9,16,16,128]{3,2,1,0:T(8,128)}, u32[]{:S(2)}) copy-start(f32[9,16,16,128]{3,2,1,0:T(8,128)} %state.7) | copy-start | bytes 3538948
  1.3 9.0 %copy-start.4 = (s32[2,2,64,32]{2,3,1,0:T(8,128)S(1)}, s32[2,2,64,32]{2,3,1,0:T(8,128)}, u32[]{:S(2)}) copy-start(s32[2,2,64,32]{2,3,1,0:T(8,128)} %param.6) | copy-start | bytes 98308
  1.3 9.1 %copy-start.1 = (f32[9,16,16,128]{3,2,1,0:T(8,128)S(1)}, f32[9,16,16,128]{3,2,1,0:T(8,128)}, u32[]{:S(2)}) copy-start(f32[9,16,16,128]{3,2,1,0:T(8,128)} %state.7) | copy-start | bytes 3538948
  1.3 9.1 %copy-start.2 = (f32[8]{0:T(128)S(1)}, f32[8]{0:T(128)}, u32[]{:S(2)}) copy-start(f32[8]{0:T(128)} %mobility.5) | copy-start | bytes 100
  1.3 9.1 %copy-start.3 = (s32[2]{0:T(128)S(1)}, s32[2]{0:T(128)}, u32[]{:S(2)}) copy-start(s32[2]{0:T(128)} %shifts.5) | copy-start | bytes 28
  1.4 13.8 %collective-permute-start.2 = (f32[9,8,8,128]{3,2,1,0:T(8,128)S(1)}, f32[9,8,8,128]{3,2,1,0:T(8,128)S(1)}, u32[]{:S(2)}, u32[]{:S(2)}) collective-permute-start(f32[9,8,8,128]{3,2,1,0:T(8,128)S(1)} %get-tuple-element.20), channel_id=1, source_target_pairs={{0,4},{4,0},{1,5},{5,1},{2,6},{6,2},{3,7},{7,3},{8,12},{12,8},{9,1... | collective-permute-start | bytes 884744 | tf_op jit(solution)/shard_map/ppermute | solution.py:506
  4.4 10.7 %collective-permute-start.1 = (f32[9,2,16,128]{3,2,1,0:T(8,128)S(1)}, f32[9,2,16,128]{3,2,1,0:T(8,128)S(1)}, u32[]{:S(2)}, u32[]{:S(2)}) collective-permute-start(f32[9,2,16,128]{3,2,1,0:T(8,128)S(1)} %shard_map.48), channel_id=1, source_target_pairs={{8,16},{24,0},{16,8},{0,24},{9,17},{25,1},{17,9},{1,25},{10,18},{2... | collective-permute-start | bytes 442376 | tf_op jit(solution)/shard_map/ppermute | solution.py:466
  7.8 7.3 %collective-permute-start = (f32[9,2,16,128]{3,2,1,0:T(8,128)S(1)}, f32[9,2,16,128]{3,2,1,0:T(8,128)S(1)}, u32[]{:S(2)}, u32[]{:S(2)}) collective-permute-start(f32[9,2,16,128]{3,2,1,0:T(8,128)S(1)} %get-tuple-element.19), channel_id=1, source_target_pairs={{0,8},{16,24},{8,0},{24,16},{1,9},{17,25},{9,1},{25,17},{2,10},{18... | collective-permute-start | bytes 442376 | tf_op jit(solution)/shard_map/ppermute | solution.py:466
  7.8 7.3 %collective-permute-start.3 = (f32[3,8,128]{2,1,0:T(8,128)S(1)}, f32[3,8,128]{2,1,0:T(8,128)S(1)}, u32[]{:S(2)}, u32[]{:S(2)}) collective-permute-start(f32[3,8,128]{2,1,0:T(8,128)S(1)} %get-tuple-element.21), channel_id=1, source_target_pairs={{0,12},{4,8},{8,4},{12,0},{16,28},{20,24},{24,20},{28,16},{1,13},{... | collective-permute-start | bytes 36872 | tf_op jit(solution)/shard_map/ppermute | solution.py:472
  9.2 5.9 %collective-permute-start.4 = (f32[3,8,128]{2,1,0:T(8,128)S(1)}, f32[3,8,128]{2,1,0:T(8,128)S(1)}, u32[]{:S(2)}, u32[]{:S(2)}) collective-permute-start(f32[3,8,128]{2,1,0:T(8,128)S(1)} %get-tuple-element.22), channel_id=1, source_target_pairs={{0,28},{4,24},{8,20},{12,16},{16,12},{20,8},{24,4},{28,0},{1,29},{... | collective-permute-start | bytes 36872 | tf_op jit(solution)/shard_map/ppermute | solution.py:472
  15.5 7.7 %collective-permute-start.5 = (f32[9,24,128]{2,1,0:T(8,128)S(1)}, f32[9,24,128]{2,1,0:T(8,128)S(1)}, u32[]{:S(2)}, u32[]{:S(2)}) collective-permute-start(f32[9,24,128]{2,1,0:T(8,128)S(1)} %shard_map.50.slab), channel_id=1, source_target_pairs={{1,0},{2,1},{3,2},{5,4},{6,5},{7,6},{9,8},{10,9},{11,10},{13,12},{... | collective-permute-start | bytes 331784 | tf_op jit(solution)/shard_map/ppermute | solution.py:525
